TPU v7x, 32 devices: a whole 2x2x4 slice. The times are simulated.
32 devices in a mesh: dom: 8 (over y, x, core), dim: 4 (over z).
Axes of the slice: x: 2, y: 2, z: 4, core: 2. Of those that a mesh axis runs over, the one named last changes fastest.
Arguments:
- particles: float32 [64, 1024], P('dom', 'dim'), may hold values from -5 to 5
- data_rows: bfloat16 [64, 16, 1024], P('dom', None, 'dim'), may hold values from -0.375 to 0.375
- labels: int32 [64, 16], P('dom'), may hold values from 0 to 1
Outputs:
- updates: float32 [2, 64, 1024], P(None, 'dom', 'dim')
All inputs are finite; a program needn't handle non-finite values.
Results may differ from a plain program's by a relative error of at most 0.0003.
Values may be sent and summed in bfloat16 or wider, within the bound.
A program may use at most 64 MiB of HBM per device.

v0:
```python
import functools

import jax
import jax.numpy as jnp
from jax import lax
from jax.experimental import pallas as pl
from jax.experimental.pallas import tpu as pltpu
from jax.sharding import PartitionSpec as P

NEWTON = 2
BAND = 1
LANES = 128

prior_precision = 0.05
like_weight = 4.0
move_size = 0.5
MESH = pl.DeviceIdType.MESH
f32 = jnp.float32
bf16 = jnp.bfloat16


def halves(v):
    high = v.astype(bf16).astype(f32)
    return jnp.concatenate([high, v - high], axis=0).astype(bf16)


def fold(product):
    rows = product.shape[0] // 2
    return product[:rows] + product[rows:]


def dot(a, b):
    return lax.dot_general(a, b, (((1,), (0,)), ((), ())), preferred_element_type=f32)


def dot_t(a, b):
    return lax.dot_general(a, b, (((1,), (1,)), ((), ())), preferred_element_type=f32)


def steps(
    nd, nz, x_ref, a_ref, y_ref, out_ref,
    basis, spread, xbuf, dist, lgt, proj, rough, marked, sums, moves, cross_terms,
    a_send, a_recv, x_send, x_recv, d_send, d_recv, l_send, l_recv, p_send, p_recv,
    r_send, r_recv, m_send, m_recv, s_send, s_recv,
    b_send, b_recv, h_send, h_recv, g_send, g_recv,
):
    rows, width = x_ref.shape
    draws = a_ref.shape[0]
    per_row = draws // rows
    count = nd * rows
    wide = dist.shape[-1]
    cols = nd * draws
    scale = 1.0 * BAND * width * nz
    cross = 4.0 / (scale * scale)
    me_dom = lax.axis_index("dom")
    me_dim = lax.axis_index("dim")
    chips = nd // 2
    chip, core = me_dom // 2, me_dom % 2
    dom_to = [((chip + m // 2) % chips) * 2 + (core + m) % 2 for m in range(nd)]
    upper = (me_dim * 2) // nz

    def dom_copy(m, src, dst, send, recv):
        return pltpu.make_async_remote_copy(
            src_ref=src, dst_ref=dst(m), send_sem=send(m), recv_sem=recv(m),
            device_id={"dom": dom_to[m]}, device_id_type=MESH,
        )

    def send_dom(*what):
        copies = [dom_copy(m, *what) for m in range(1, nd)]
        for copy in copies:
            copy.start()
        return copies

    def send_dim(src, dst, send, recv):
        def one(k):
            return pltpu.make_async_remote_copy(
                src_ref=src, dst_ref=dst(k), send_sem=send(k), recv_sem=recv(k),
                device_id={"dim": lax.rem(me_dim + k, nz)}, device_id_type=MESH,
            )

        for k in range(1, nz):
            one(upper * k + (1 - upper) * (nz - k)).start()
        return [one(k) for k in range(1, nz)]

    barrier = pltpu.get_barrier_semaphore()
    for k in range(1, nd):
        pl.semaphore_signal(barrier, inc=1, device_id={"dom": dom_to[k]}, device_id_type=MESH)
    for k in range(1, nz):
        pl.semaphore_signal(barrier, inc=1, device_id={"dim": lax.rem(me_dim + k, nz)}, device_id_type=MESH)

    lane_of = lax.broadcasted_iota(jnp.int32, (rows, draws), 1) // per_row
    row_of = lax.broadcasted_iota(jnp.int32, (rows, draws), 0)
    own_block = lane_of == row_of

    def flat(values):
        return jnp.sum(jnp.where(own_block, values, 0.0), axis=0, keepdims=True)

    basis[0:draws, :] = a_ref[...]
    tile = lax.broadcasted_iota(jnp.int32, (per_row, draws), 1) % per_row
    tile = (tile == lax.broadcasted_iota(jnp.int32, (per_row, draws), 0)).astype(f32).astype(bf16)
    labels = flat(dot(y_ref[...].astype(f32).astype(bf16), tile))
    current = x_ref[...]
    pending = []
    first_eight = lax.broadcasted_iota(jnp.int32, (rows, count), 1)
    own_pair = first_eight == lax.broadcasted_iota(jnp.int32, (rows, count), 0)
    lane = lax.broadcasted_iota(jnp.int32, (rows, LANES), 1)

    def paired(product):
        return product[:, : product.shape[1] // 2] + product[:, product.shape[1] // 2 :]

    def column_sums(values):
        return paired(dot_t(jnp.ones((rows, width), bf16), halves(values)))

    def row_sums(values):
        return jnp.sum(values, axis=1, keepdims=True)

    xbuf[0, :, 0:width] = current
    xbuf[0, 0:1, width:] = flat(fold(dot_t(halves(current), a_ref[...])))
    xbuf[0, 1:2, width:] = labels
    pl.semaphore_wait(barrier, nd - 1 + nz - 1)
    copies = send_dom(xbuf.at[0], lambda k: xbuf.at[k], lambda k: x_send.at[k], lambda k: x_recv.at[k])
    pending += copies
    a_parts = (
        lambda k: basis.at[pl.ds(k * draws, draws), :], lambda k: a_send.at[k], lambda k: a_recv.at[k],
    )
    a_far = [dom_copy(m, a_ref, *a_parts) for m in range(2, nd, 2)]
    a_near = [dom_copy(1, a_ref, *a_parts)]
    for copy in a_far + a_near:
        copy.start()
    spread_col = lax.broadcasted_iota(jnp.int32, spread.shape, 1) // per_row
    spread_row = lax.broadcasted_iota(jnp.int32, spread.shape, 0)
    spread[...] = (spread_col == spread_row).astype(f32).astype(bf16)
    for copy in copies:
        copy.wait_recv()
    everyone = xbuf[:, :, 0:width].reshape(count, width)
    pieces = halves(everyone)
    basis[cols:, :] = pieces
    for k in range(nd):
        lgt[0, k : k + 1, :] = xbuf[k, 0:1, width:]
    inner = paired(fold(dot_t(halves(current), pieces)))
    dist[0, :, 0:count] = row_sums(current * current) + column_sums(everyone * everyone) - 2.0 * inner
    if wide > count:
        dist[0, :, count:] = jnp.zeros((rows, wide - count), f32)
    c1 = send_dim(dist.at[0], lambda k: dist.at[k], lambda k: d_send.at[k], lambda k: d_recv.at[k])
    c2 = send_dim(lgt.at[0], lambda k: lgt.at[k], lambda k: l_send.at[k], lambda k: l_recv.at[k])
    pending += c1 + c2
    for m, copy in zip(range(2, nd, 2), a_far):
        copy.wait_recv()
        on = pltpu.make_async_remote_copy(
            src_ref=basis.at[pl.ds(m * draws, draws), :], dst_ref=basis.at[pl.ds((m + 1) * draws, draws), :],
            send_sem=a_send.at[m + 1], recv_sem=a_recv.at[m + 1],
            device_id={"dom": dom_to[1]}, device_id_type=MESH,
        )
        on.start()
        a_near.append(on)
    pending += a_far + a_near
    for copy in c1 + c2:
        copy.wait_recv()
    distance = functools.reduce(jnp.add, [dist[k] for k in range(nz)])[:, :count]
    logits = functools.reduce(jnp.add, [lgt[k] for k in range(nz)])

    for t in range(NEWTON):
        last = t + 1 == NEWTON
        prob = 1.0 / (1.0 + jnp.exp(-logits))
        curve = like_weight * prob * (1.0 - prob)
        kernel = jnp.exp(-distance / scale)
        kernel_sq = kernel * kernel
        total = jnp.sum(kernel, axis=1, keepdims=True)
        total_sq = jnp.sum(kernel_sq, axis=1, keepdims=True)
        both = jnp.concatenate([kernel, kernel_sq], axis=0)
        wider = fold(dot(halves(both), spread[...]))
        kernel_wide, kernel_sq_wide = wider[:rows], wider[rows:]
        weight, drive = [], []
        for k in range(nd):
            part = slice(k * draws, (k + 1) * draws)
            gap = like_weight * (xbuf[k, 1:2, width:] - prob[k : k + 1])
            drive.append(kernel_wide[:, part] * gap)
            weight.append(kernel_sq_wide[:, part] * curve[k : k + 1])
        weight = jnp.concatenate(weight, axis=1)
        drive = jnp.concatenate(drive, axis=1)
        if t == 0:
            for copy in a_near:
                copy.wait_recv()
        pull = (-prior_precision - 2.0 / scale) * kernel

        def back(on_rows, on_x):
            return fold(dot(halves(jnp.concatenate([on_rows, on_x, on_x], axis=1)), basis[...]))

        def ahead(vectors):
            out = fold(dot_t(halves(vectors), basis[...]))
            parts = [out[:, :cols], out[:, cols : cols + count] + out[:, cols + count :]]
            if wide > count:
                parts.append(jnp.zeros((rows, wide - count), f32))
            return jnp.concatenate(parts, axis=1)

        def own_dots(along):
            return jnp.sum(jnp.where(own_pair, along, 0.0), axis=1, keepdims=True)

        drift = (back(drive, pull) + (2.0 / scale) * total * current) / count
        proj[t, 0] = ahead(drift)
        copies = send_dim(proj.at[t, 0], lambda k: proj.at[t, k], lambda k: p_send.at[t, k], lambda k: p_recv.at[t, k])
        pending += copies
        if not last:
            moves[t, 0, 0] = drift
            b_copies = send_dom(
                moves.at[t, 0, 0], lambda k: moves.at[t, 0, k], lambda k: b_send.at[t, k], lambda k: b_recv.at[t, k]
            )
            pending += b_copies
        for copy in copies:
            copy.wait_recv()
        seen = functools.reduce(jnp.add, [proj[t, k] for k in range(nz)])
        drift_logits = flat(seen[:, :draws])
        along = seen[:, cols : cols + count]
        on_x = cross * kernel_sq * (along - own_dots(along))
        image = back(weight * seen[:, :cols], on_x)
        image = image + prior_precision * total_sq * drift - jnp.sum(on_x, axis=1, keepdims=True) * current
        image = image / count
        if not last:
            moves[t, 1, 0] = image
            h_copies = send_dom(
                moves.at[t, 1, 0], lambda k: moves.at[t, 1, k], lambda k: h_send.at[t, k], lambda k: h_recv.at[t, k]
            )
            pending += h_copies
        exact = ahead(image)
        rough[t, 0] = exact.astype(bf16)
        c1 = send_dim(rough.at[t, 0], lambda k: rough.at[t, k], lambda k: r_send.at[t, k], lambda k: r_recv.at[t, k])
        image_sq = jnp.sum(image * image, axis=1, keepdims=True)
        marks = jnp.where(lane == 0, jnp.sum(drift * drift, axis=1, keepdims=True), 0.0)
        marks = jnp.where(lane == 1, jnp.sum(drift * image, axis=1, keepdims=True), marks)
        marks = jnp.where(lane == 2, image_sq, marks)
        marks = jnp.where(lane == 3, prior_precision * total_sq * image_sq, marks)
        marked[t, 0] = jnp.concatenate(
            [jnp.sum(marks, axis=0, keepdims=True), flat(exact[:, :draws]), jnp.zeros((rows - 2, LANES), f32)], axis=0
        )
        c2 = send_dim(marked.at[t, 0], lambda k: marked.at[t, k], lambda k: m_send.at[t, k], lambda k: m_recv.at[t, k])
        pending += c1 + c2
        if not last:
            for copy in b_copies + h_copies:
                copy.wait_recv()
            every = [everyone, moves[t, 0].reshape(count, width), moves[t, 1].reshape(count, width)]
            own = [current, drift, image]
            pairs = [(0, 1), (0, 2), (1, 1), (1, 2), (2, 2)]
            own_pieces = halves(jnp.concatenate(own, axis=0))
            inner = [paired(fold(dot_t(own_pieces, halves(v)))) for v in every]
            square = column_sums(jnp.concatenate([every[u] * every[v] for u, v in pairs], axis=0))
            terms = []
            for n, (u, v) in enumerate(pairs):
                mixed = inner[v][u * rows : (u + 1) * rows] + inner[u][v * rows : (v + 1) * rows]
                terms.append(row_sums(own[u] * own[v]) + square[:, n * count : (n + 1) * count] - mixed)
            spare = cross_terms.shape[-1] - len(pairs) * count
            if spare > 0:
                terms.append(jnp.zeros((rows, spare), f32))
            cross_terms[t, 0] = jnp.concatenate(terms, axis=1)
            g_copies = send_dim(
                cross_terms.at[t, 0], lambda k: cross_terms.at[t, k], lambda k: g_send.at[t, k], lambda k: g_recv.at[t, k]
            )
            pending += g_copies
        for copy in c1 + c2:
            copy.wait_recv()
        seen = functools.reduce(jnp.add, [rough[t, k].astype(f32) for k in range(1, nz)], exact)
        along = seen[:, cols : cols + count]
        gap = along - own_dots(along)
        bent = jnp.sum(weight * seen[:, :cols] * seen[:, :cols], axis=1, keepdims=True)
        bent = bent + cross * jnp.sum(kernel_sq * gap * gap, axis=1, keepdims=True)
        marks = functools.reduce(jnp.add, [marked[t, k] for k in range(nz)])
        bent = jnp.sum(bent, axis=0, keepdims=True)
        sums[t, 0] = jnp.concatenate(
            [marks[0:1] + jnp.where(lane[0:1] == 3, bent, 0.0), drift_logits, marks[1:2], marks[3:]], axis=0
        )
        copies = send_dom(
            sums.at[t, 0], lambda k: sums.at[t, k], lambda k: s_send.at[t, k], lambda k: s_recv.at[t, k]
        )
        pending += copies
        for copy in copies:
            copy.wait_recv()
        marks = functools.reduce(jnp.add, [sums[t, k, 0:1] for k in range(nd)])
        first = lax.broadcasted_iota(jnp.int32, (1, LANES), 1)
        norm, curve_total, image_square, bent = [
            jnp.sum(jnp.where(first == k, marks, 0.0), axis=1, keepdims=True) for k in range(4)
        ]
        bent = bent / count
        alpha = norm / curve_total
        norm_next = norm - 2.0 * alpha * curve_total + alpha * alpha * image_square
        keep = 1.0 + norm_next / norm
        curve_next = keep * keep * curve_total - 2.0 * keep * alpha * image_square + alpha * alpha * bent
        alpha_next = norm_next / curve_next
        on_drift, on_image = alpha + alpha_next * keep, -alpha_next * alpha
        update = on_drift * drift + on_image * image
        out_ref[t] = update
        if not last:
            current = current + move_size * update
            step_b, step_h = move_size * on_drift, move_size * on_image
            everyone = everyone + step_b * every[1] + step_h * every[2]
            basis[cols:, :] = halves(everyone)
            shifts = [sums[t, k, 1:2] * step_b + sums[t, k, 2:3] * step_h for k in range(nd)]
            logits = logits + jnp.concatenate(shifts, axis=0)
            for copy in g_copies:
                copy.wait_recv()
            terms = functools.reduce(jnp.add, [cross_terms[t, k] for k in range(nz)])
            by = [2.0 * step_b, 2.0 * step_h, step_b * step_b, 2.0 * step_b * step_h, step_h * step_h]
            for n, factor in enumerate(by):
                distance = distance + factor * terms[:, n * count : (n + 1) * count]
    for copy in pending:
        copy.wait_send()


def solution(mesh):
    nd, nz = mesh.shape["dom"], mesh.shape["dim"]

    def per_device(particles, data_rows, labels):
        rows, width = particles.shape
        draws = data_rows.shape[0] * data_rows.shape[1]
        count = nd * rows
        wide = -(-count // LANES) * LANES
        cols = nd * draws
        dma = pltpu.SemaphoreType.DMA
        over_dom, over_dim = (NEWTON, nd), (NEWTON, nz)
        pairs = [(nd,), (nd,), (nz,), (nz,)] + [over_dim] * 3 + [over_dom] * 3 + [over_dim]
        return pl.pallas_call(
            functools.partial(steps, nd, nz),
            out_shape=jax.ShapeDtypeStruct((NEWTON, rows, width), f32),
            in_specs=[pl.BlockSpec(memory_space=pltpu.VMEM)] * 3,
            out_specs=pl.BlockSpec(memory_space=pltpu.VMEM),
            scratch_shapes=[
                pltpu.VMEM((cols + 2 * count, width), bf16),
                pltpu.VMEM((count, cols), bf16),
                pltpu.VMEM((nd, rows, width + draws), f32),
                pltpu.VMEM((nz, rows, wide), f32),
                pltpu.VMEM((nz, nd, draws), f32),
                pltpu.VMEM((NEWTON, nz, rows, cols + wide), f32),
                pltpu.VMEM((NEWTON, nz, rows, cols + wide), bf16),
                pltpu.VMEM((NEWTON, nz, rows, LANES), f32),
                pltpu.VMEM((NEWTON, nd, rows, LANES), f32),
                pltpu.VMEM((NEWTON, 2, nd, rows, width), f32),
                pltpu.VMEM((NEWTON, nz, rows, -(-5 * count // LANES) * LANES), f32),
            ]
            + [dma(shape) for shape in pairs for _ in range(2)],
            compiler_params=pltpu.CompilerParams(collective_id=0, has_side_effects=True),
        )(particles, data_rows.reshape(draws, width), labels)

    placed = (P("dom", "dim"), P("dom", None, "dim"), P("dom", None))
    return jax.shard_map(
        per_device, mesh=mesh, in_specs=placed, out_specs=P(None, "dom", "dim"), check_vma=False
    )
```

profile of v0, /device:TPU:1, one launch (start us, length us, event | category | flops | bytes accessed | tf_op | source)
XLA Modules:
  0.0 43.9 jit_solution(1801213143807143472)
XLA Ops:
  0.0 42.6 %shard_map.37 = f32[2,8,256]{2,1,0:T(8,128)} custom-call(f32[8,256]{1,0:T(8,128)} %x_ref.1, bf16[128,256]{1,0:T(8,128)(2,1)} %bitcast.1, s32[8,16]{1,0:T(8,128)} %y_ref.1), custom_call_target="tpu_custom_call" | custom-call | tf_op jit(solution)/shard_map/pallas_call | solution.py:319
  42.6 1.3 %copy.5 = f32[2,8,256]{2,1,0:T(8,128)} copy(f32[2,8,256]{2,1,0:T(8,128)} %shard_map.37) | data formatting | bytes 32768
where the time goes:
time: 44.6 us; the launch traced here: 43.9 us
  Pallas kernels  42.6 us (96%)
  local copies, waits for them, and re-layouts  1.32 us (3%)
    pallas_call x1, Pallas kernels, per_device(): pl.pallas_call(functools.partial(steps, nd, nz), out_shape=jax.ShapeDtype...  42.6 us
    unnamed x1, local copies, waits for them, and re-layouts  1.32 us

commit v1 on v0

v1 whole, which is shorter than its diff:
```python
import functools

import jax
import jax.numpy as jnp
from jax import lax
from jax.experimental import pallas as pl
from jax.experimental.pallas import tpu as pltpu
from jax.sharding import PartitionSpec as P

NEWTON = 2
BAND = 1
LANES = 128

prior_precision = 0.05
like_weight = 4.0
move_size = 0.5
MESH = pl.DeviceIdType.MESH
f32 = jnp.float32
bf16 = jnp.bfloat16


def halves(v):
    high = v.astype(bf16).astype(f32)
    return jnp.concatenate([high, v - high], axis=0).astype(bf16)


def fold(product):
    rows = product.shape[0] // 2
    return product[:rows] + product[rows:]


def paired(product):
    half = product.shape[1] // 2
    return product[:, :half] + product[:, half:]


def dot(a, b):
    return lax.dot_general(a, b, (((1,), (0,)), ((), ())), preferred_element_type=f32)


def dot_t(a, b):
    return lax.dot_general(a, b, (((1,), (1,)), ((), ())), preferred_element_type=f32)


def total_of(values):
    return jnp.sum(jnp.sum(values, axis=0, keepdims=True), axis=1, keepdims=True)


def steps(
    nd, nz, x_ref, a_ref, y_ref, out_ref,
    rows_all, xbuf, xpieces, upd,
    x_recv, xd_recv, a_recv, ad_recv, send,
):
    rows, width = x_ref.shape
    draws = a_ref.shape[0]
    per_row = draws // rows
    chips = nd // 2
    count = nd * rows
    cols = nd * draws
    scale = 1.0 * BAND * width * nz
    cross = 4.0 / (scale * scale)
    me_dom = lax.axis_index("dom")
    z = lax.axis_index("dim")
    chip, core = me_dom // 2, me_dom % 2
    relay = chips == 4

    if relay:
        near = [chip + 1 - 2 * (chip % 2), chip + 2 - 4 * (chip // 2), 3 - chip]
    else:
        near = [(chip + m) % chips for m in range(1, chips)]
    if nz == 4:
        high = z // 2
        zs = [z + 1 - 2 * (z % 2), 2 - high, 3 - 3 * high]
    else:
        zs = [(z + k) % nz for k in range(1, nz)]
    planes = [z] + zs

    sent = []

    def copy(src, dst, recv, device):
        one = pltpu.make_async_remote_copy(
            src_ref=src, dst_ref=dst, send_sem=send.at[len(sent)], recv_sem=recv,
            device_id=device, device_id_type=MESH,
        )
        one.start()
        sent.append(one)

    def wait(dst, recv):
        pltpu.make_async_remote_copy(
            src_ref=dst, dst_ref=dst, send_sem=send.at[0], recv_sem=recv,
            device_id={"dom": me_dom + 1 - 2 * core}, device_id_type=MESH,
        ).wait_recv()

    def on_chip(c):
        return {"dom": c * 2 + core}

    partner = {"dom": me_dom + 1 - 2 * core}

    def xs(plane, c):
        return xbuf.at[plane, core, c]

    def whole(plane, c):
        return rows_all.at[plane, core, c]

    def part(plane, c, h):
        return rows_all.at[plane, core, c, pl.ds(h * (draws // 2), draws // 2)]

    barrier = pltpu.get_barrier_semaphore()
    greet = [on_chip(c) for c in near] + [{"dim": k} for k in zs] + [partner]
    for device in greet:
        pl.semaphore_signal(barrier, inc=1, device_id=device, device_id_type=MESH)

    lane_of = lax.broadcasted_iota(jnp.int32, (rows, draws), 1) // per_row
    row_of = lax.broadcasted_iota(jnp.int32, (rows, draws), 0)
    own_block = lane_of == row_of

    def flat(values):
        return jnp.sum(jnp.where(own_block, values, 0.0), axis=0, keepdims=True)

    tile = lax.broadcasted_iota(jnp.int32, (per_row, draws), 1) % per_row
    tile = (tile == lax.broadcasted_iota(jnp.int32, (per_row, draws), 0)).astype(f32).astype(bf16)
    labels = flat(dot(y_ref[...].astype(f32).astype(bf16), tile))
    own_x = x_ref[...]
    first = flat(fold(dot_t(halves(own_x), a_ref[...])))
    xbuf[z, core, chip, :, 0:width] = own_x
    xbuf[z, core, chip, :, width:] = jnp.concatenate([first, labels, jnp.zeros((rows - 2, draws), f32)], axis=0)
    rows_all[z, core, chip] = a_ref[...]
    pl.semaphore_wait(barrier, len(greet))

    for k in zs:
        copy(xs(z, chip), xs(z, chip), x_recv.at[z, chip], {"dim": k})
    for c in near:
        copy(xs(z, chip), xs(z, chip), x_recv.at[z, chip], on_chip(c))
    reach = near[:2] if relay else near
    for c in reach:
        copy(a_ref, whole(z, chip), a_recv.at[z, chip, 0], on_chip(c))
    for k in zs:
        copy(a_ref, whole(z, chip), a_recv.at[z, chip, 0], {"dim": k})

    def x_forward(plane):
        wait(xs(plane, chip), x_recv.at[plane, chip])
        for c in near:
            copy(xs(plane, chip), xs(plane, chip), x_recv.at[plane, chip], on_chip(c))

    def x_across(plane):
        for c in near:
            wait(xs(plane, c), x_recv.at[plane, c])
        copy(xbuf.at[plane, core], xbuf.at[plane, core], xd_recv.at[plane], partner)

    def a_forward(plane):
        wait(whole(plane, chip), a_recv.at[plane, chip, 0])
        for c in reach:
            copy(whole(plane, chip), whole(plane, chip), a_recv.at[plane, chip, 0], on_chip(c))

    def a_relay(plane):
        for m, c in enumerate(reach):
            wait(whole(plane, c), a_recv.at[plane, c, 0])
            if relay:
                copy(part(plane, c, m), part(plane, c, m), a_recv.at[plane, c, m], on_chip(near[1 - m]))

    def a_across(plane):
        if relay:
            for h in range(2):
                wait(part(plane, near[2], h), a_recv.at[plane, near[2], h])
        copy(rows_all.at[plane, core], rows_all.at[plane, core], ad_recv.at[plane], partner)

    for plane in zs:
        x_forward(plane)
    a_relay(z)
    x_across(z)
    for n, plane in enumerate(zs):
        a_forward(plane)
        if n == 0:
            x_across(plane)
            a_across(z)
        else:
            a_relay(zs[n - 1])
            x_across(plane)
            a_across(zs[n - 1])
    if nz > 1:
        a_relay(zs[-1])
        a_across(zs[-1])

    for plane in planes:
        wait(xbuf.at[plane, 1 - core], xd_recv.at[plane])
    eye = lax.broadcasted_iota(jnp.int32, (count, count), 1) == lax.broadcasted_iota(jnp.int32, (count, count), 0)
    for k in range(nz):
        upd[2, k] = xbuf[k, :, :, :, 0:width].reshape(count, width)

    def piece_x():
        for k in range(nz):
            xpieces[:, k * width : (k + 1) * width] = halves(upd[2, k])

    def row_sums(values):
        return jnp.sum(values, axis=1, keepdims=True)

    marks = functools.reduce(jnp.add, [xbuf[k, :, :, :, width:].reshape(count, draws) for k in range(nz)])
    targets = xbuf[0, :, :, :, width:].reshape(count, draws)
    logits = jnp.concatenate([marks[g * rows : g * rows + 1] for g in range(nd)], axis=0)
    targets = jnp.concatenate([targets[g * rows + 1 : g * rows + 2] for g in range(nd)], axis=0)
    spread_at = lax.broadcasted_iota(jnp.int32, (count, LANES), 1) // per_row
    for plane in planes:
        wait(rows_all.at[plane, 1 - core], ad_recv.at[plane])

    def back(on_rows, on_x):
        left = halves(on_rows)
        left_x = halves(jnp.concatenate([on_x, on_x], axis=1))
        parts = []
        for k in range(nz):
            product = dot(left, rows_all[k].reshape(cols, width))
            product = product + dot(left_x, xpieces[:, k * width : (k + 1) * width])
            parts.append(fold(product))
        return parts

    def ahead(parts):
        pieces = [halves(v) for v in parts]
        seen = functools.reduce(jnp.add, [dot_t(pieces[k], rows_all[k].reshape(cols, width)) for k in range(nz)])
        along = functools.reduce(
            jnp.add, [dot_t(pieces[k], xpieces[:, k * width : (k + 1) * width]) for k in range(nz)]
        )
        return fold(seen), paired(fold(along))

    def own_logits(seen):
        return jnp.concatenate(
            [flat(seen[g * rows : (g + 1) * rows, g * draws : (g + 1) * draws]) for g in range(nd)], axis=0
        )

    for t in range(NEWTON):
        last = t + 1 == NEWTON
        piece_x()
        inner = paired(fold(dot_t(xpieces[...], xpieces[...])))
        diagonal = jnp.where(eye, inner, 0.0)
        distance = row_sums(diagonal) + jnp.sum(diagonal, axis=0, keepdims=True) - 2.0 * inner
        kernel = jnp.exp(distance * (-1.0 / scale))
        prob = 1.0 / (1.0 + jnp.exp(-logits))
        curve = like_weight * prob * (1.0 - prob)
        gap = like_weight * (targets - prob)
        kernel_sq = kernel * kernel
        total = row_sums(kernel)
        total_sq = row_sums(kernel_sq)
        padded = kernel
        if count < LANES:
            padded = jnp.concatenate([kernel, jnp.zeros((count, LANES - count), f32)], axis=1)
        drive, weight = [], []
        for g in range(nd):
            at = g * rows
            block = padded[:, at // LANES * LANES : at // LANES * LANES + LANES]
            wide = jnp.take_along_axis(block, spread_at + at % LANES, axis=1)
            drive.append(wide * gap[g : g + 1])
            weight.append(wide * wide * curve[g : g + 1])
        drive = jnp.concatenate(drive, axis=1)
        weight = jnp.concatenate(weight, axis=1)
        pull = (-prior_precision - 2.0 / scale) * kernel + jnp.where(eye, (2.0 / scale) * total, 0.0)
        drift = [v / count for v in back(drive, pull)]
        seen, along = ahead(drift)
        shift = own_logits(seen)
        on_x = cross * kernel_sq * (along - row_sums(jnp.where(eye, along, 0.0)))
        on_x = on_x - jnp.where(eye, row_sums(on_x), 0.0)
        image = back(weight * seen, on_x)
        image = [(v + prior_precision * total_sq * d) / count for v, d in zip(image, drift)]
        seen, along = ahead(image)
        shift_image = own_logits(seen)
        along = along - row_sums(jnp.where(eye, along, 0.0))
        norm = total_of(functools.reduce(jnp.add, [d * d for d in drift]))
        curve_total = total_of(functools.reduce(jnp.add, [d * v for d, v in zip(drift, image)]))
        squares = functools.reduce(jnp.add, [v * v for v in image])
        image_square = total_of(squares)
        bent = total_of(prior_precision * total_sq * row_sums(squares) + cross * row_sums(kernel_sq * along * along))
        bent = (bent + total_of(weight * seen * seen)) / count
        alpha = norm / curve_total
        norm_next = norm - 2.0 * alpha * curve_total + alpha * alpha * image_square
        keep = 1.0 + norm_next / norm
        curve_next = keep * keep * curve_total - 2.0 * keep * alpha * image_square + alpha * alpha * bent
        alpha_next = norm_next / curve_next
        on_drift, on_image = alpha + alpha_next * keep, -alpha_next * alpha
        for k in range(nz):
            update = on_drift * drift[k] + on_image * image[k]
            upd[t, k] = update
            if not last:
                upd[2, k] = upd[2, k] + move_size * update
        if not last:
            logits = logits + move_size * (on_drift * shift + on_image * shift_image)
        out_ref[t] = upd[t, z, pl.ds(pl.multiple_of((core * chips + chip) * rows, rows), rows), :]
    for one in sent:
        one.wait_send()


def solution(mesh):
    nd, nz = mesh.shape["dom"], mesh.shape["dim"]

    def per_device(particles, data_rows, labels):
        rows, width = particles.shape
        draws = data_rows.shape[0] * data_rows.shape[1]
        count = nd * rows
        chips = nd // 2
        reach = 2 if chips == 4 else chips - 1
        number = (chips - 1 + nz - 1) + (reach + nz - 1) + (nz - 1) * (chips - 1 + reach) + 2 * nz
        if chips == 4:
            number += 2 * nz
        dma = pltpu.SemaphoreType.DMA
        return pl.pallas_call(
            functools.partial(steps, nd, nz),
            out_shape=jax.ShapeDtypeStruct((NEWTON, rows, width), f32),
            in_specs=[pl.BlockSpec(memory_space=pltpu.VMEM)] * 3,
            out_specs=pl.BlockSpec(memory_space=pltpu.VMEM),
            scratch_shapes=[
                pltpu.VMEM((nz, 2, chips, draws, width), bf16),
                pltpu.VMEM((nz, 2, chips, rows, width + draws), f32),
                pltpu.VMEM((2 * count, nz * width), bf16),
                pltpu.VMEM((NEWTON + 1, nz, count, width), f32),
                dma((nz, chips)),
                dma((nz,)),
                dma((nz, chips, 2)),
                dma((nz,)),
                dma((number,)),
            ],
            compiler_params=pltpu.CompilerParams(collective_id=0, has_side_effects=True),
        )(particles, data_rows.reshape(draws, width), labels)

    placed = (P("dom", "dim"), P("dom", None, "dim"), P("dom", None))
    return jax.shard_map(
        per_device, mesh=mesh, in_specs=placed, out_specs=P(None, "dom", "dim"), check_vma=False
    )
```

time: 44.6 us -> 36.7 us (0.82)
  Pallas kernels: 42.6 us -> 35.1 us
    pallas_call x1, Pallas kernels: 42.6 us -> 35.1 us  [per_device(): pl.pallas_call(functools.partial(steps, nd, nz), out_shape=jax.ShapeDtype...]
where the time goes in v1:
time: 36.7 us; the launch traced here: 36.4 us
  Pallas kernels  35.1 us (96%)
  local copies, waits for them, and re-layouts  1.32 us (4%)
    pallas_call x1, Pallas kernels, per_device(): pl.pallas_call(functools.partial(steps, nd, nz), out_shape=jax.ShapeDtype...  35.1 us
    unnamed x1, local copies, waits for them, and re-layouts  1.32 us

profile of v1, /device:TPU:1, one launch (start us, length us, event | category | flops | bytes accessed | tf_op | source)
XLA Modules:
  0.0 36.4 jit_solution(4798693109237652786)
XLA Ops:
  0.0 35.1 %shard_map.37 = f32[2,8,256]{2,1,0:T(8,128)} custom-call(f32[8,256]{1,0:T(8,128)} %x_ref.1, bf16[128,256]{1,0:T(8,128)(2,1)} %bitcast.1, s32[8,16]{1,0:T(8,128)} %y_ref.1), custom_call_target="tpu_custom_call" | custom-call | tf_op jit(solution)/shard_map/pallas_call | solution.py:301
  35.1 1.3 %copy.5 = f32[2,8,256]{2,1,0:T(8,128)} copy(f32[2,8,256]{2,1,0:T(8,128)} %shard_map.37) | data formatting | bytes 32768

commit v2 on v1

--- a/solution.py
+++ b/solution.py
@@ -49,12 +49,13 @@
 def steps(
     nd, nz, x_ref, a_ref, y_ref, out_ref,
     rows_all, xbuf, xpieces, upd,
-    x_recv, xd_recv, a_recv, ad_recv, send,
+    x_recv, x_over, a_recv, a_over, send,
 ):
     rows, width = x_ref.shape
     draws = a_ref.shape[0]
     per_row = draws // rows
     chips = nd // 2
+    slots = nz * nd
     count = nd * rows
     cols = nd * draws
     scale = 1.0 * BAND * width * nz
@@ -62,48 +63,47 @@
     me_dom = lax.axis_index("dom")
     z = lax.axis_index("dim")
     chip, core = me_dom // 2, me_dom % 2
-    relay = chips == 4
-
-    if relay:
+    square = chips == 4 and nz == 4
+
+    if square:
         near = [chip + 1 - 2 * (chip % 2), chip + 2 - 4 * (chip // 2), 3 - chip]
+        high = z // 2
+        middle = (z + 1) // 2 % 2 == 1
+        zs = [3 - 3 * high, 2 - high, z + 1 - 2 * (z % 2)]
     else:
         near = [(chip + m) % chips for m in range(1, chips)]
-    if nz == 4:
-        high = z // 2
-        zs = [z + 1 - 2 * (z % 2), 2 - high, 3 - 3 * high]
-    else:
         zs = [(z + k) % nz for k in range(1, nz)]
-    planes = [z] + zs
-
-    sent = []
-
-    def copy(src, dst, recv, device):
-        one = pltpu.make_async_remote_copy(
-            src_ref=src, dst_ref=dst, send_sem=send.at[len(sent)], recv_sem=recv,
-            device_id=device, device_id_type=MESH,
-        )
-        one.start()
-        sent.append(one)
-
-    def wait(dst, recv):
-        pltpu.make_async_remote_copy(
-            src_ref=dst, dst_ref=dst, send_sem=send.at[0], recv_sem=recv,
-            device_id={"dom": me_dom + 1 - 2 * core}, device_id_type=MESH,
-        ).wait_recv()
+    partner = {"dom": me_dom + 1 - 2 * core}
+    started = {"x": 0, "a": 0, "p": 0}
+    sems = {"x": send.at[0], "a": send.at[1], "p": send.at[2], "m": send.at[3]}
 
     def on_chip(c):
         return {"dom": c * 2 + core}
 
-    partner = {"dom": me_dom + 1 - 2 * core}
-
-    def xs(plane, c):
-        return xbuf.at[plane, core, c]
-
-    def whole(plane, c):
-        return rows_all.at[plane, core, c]
-
-    def part(plane, c, h):
-        return rows_all.at[plane, core, c, pl.ds(h * (draws // 2), draws // 2)]
+    def slot(plane, c, k=None):
+        return (plane * 2 + (core if k is None else k)) * chips + c
+
+    def copy(kind, ref, recv, device, src=None):
+        pltpu.make_async_remote_copy(
+            src_ref=ref if src is None else src, dst_ref=ref, send_sem=sems[kind], recv_sem=recv,
+            device_id=device, device_id_type=MESH,
+        ).start()
+        if kind in started:
+            started[kind] += 1
+
+    def wait(ref, recv):
+        pltpu.make_async_remote_copy(
+            src_ref=ref, dst_ref=ref, send_sem=send.at[0], recv_sem=recv, device_id=partner, device_id_type=MESH,
+        ).wait_recv()
+
+    def wait_sent(ref, kind, number):
+        while number > 0:
+            part = ref.at[pl.ds(0, min(number, slots))]
+            pltpu.make_async_remote_copy(
+                src_ref=part, dst_ref=part, send_sem=sems[kind], recv_sem=send.at[0],
+                device_id=partner, device_id_type=MESH,
+            ).wait_send()
+            number -= slots
 
     barrier = pltpu.get_barrier_semaphore()
     greet = [on_chip(c) for c in near] + [{"dim": k} for k in zs] + [partner]
@@ -122,70 +122,83 @@
     labels = flat(dot(y_ref[...].astype(f32).astype(bf16), tile))
     own_x = x_ref[...]
     first = flat(fold(dot_t(halves(own_x), a_ref[...])))
-    xbuf[z, core, chip, :, 0:width] = own_x
-    xbuf[z, core, chip, :, width:] = jnp.concatenate([first, labels, jnp.zeros((rows - 2, draws), f32)], axis=0)
-    rows_all[z, core, chip] = a_ref[...]
+    here = slot(z, chip)
+    xbuf[here, :, 0:width] = own_x
+    xbuf[here, :, width:] = jnp.concatenate([first, labels, jnp.zeros((rows - 2, draws), f32)], axis=0)
+    rows_all[here] = a_ref[...]
     pl.semaphore_wait(barrier, len(greet))
 
-    for k in zs:
-        copy(xs(z, chip), xs(z, chip), x_recv.at[z, chip], {"dim": k})
+    def send_x(plane, devices, role):
+        for device in devices:
+            copy("x", xbuf.at[slot(plane, chip)], x_recv.at[plane, role], device)
+
+    def send_a(plane, devices, role, src=None):
+        for device in devices:
+            copy("a", rows_all.at[slot(plane, chip)], a_recv.at[plane, role], device, src)
+
+    plane_devices = [on_chip(c) for c in near]
+    z_devices = [{"dim": k} for k in zs]
+    side, diagonal = (near[:2], near[2]) if square else (near, None)
+    send_x(z, z_devices, 0)
+    send_x(z, plane_devices, 1)
+    send_a(z, plane_devices[: len(side)], 1, a_ref)
+    if square:
+        send_a(z, plane_devices[2:], 2, a_ref)
+    send_a(z, z_devices, 0, a_ref)
+    for plane in zs:
+        wait(xbuf.at[slot(plane, chip)], x_recv.at[plane, 0])
+        send_x(plane, plane_devices, 1)
+
+    def across(plane, c):
+        copy("p", rows_all.at[slot(plane, c)], a_over.at[plane], partner)
+
+    for n, plane in enumerate(zs):
+        wait(rows_all.at[slot(plane, chip)], a_recv.at[plane, 0])
+        if square and n == 0:
+            send_a(plane, plane_devices[2:], 2)
+        send_a(plane, plane_devices[: len(side)], 1)
+        if square and n == 0:
+            from_corner = rows_all.at[slot(z, diagonal)]
+            wait(from_corner, a_recv.at[z, 2])
+            copy("a", from_corner, a_recv.at[z, 2], z_devices[2])
+
+            @pl.when(middle)
+            def _():
+                for device in z_devices[:2]:
+                    copy("m", from_corner, a_recv.at[z, 2], device)
+
+    for plane in [z] + zs:
+        wait(xbuf.at[pl.ds(0, len(near))], x_recv.at[plane, 1])
+        bundle = xbuf.at[pl.ds(slot(plane, 0), chips)]
+        pltpu.make_async_remote_copy(
+            src_ref=bundle, dst_ref=bundle, send_sem=sems["x"], recv_sem=x_over.at[plane],
+            device_id=partner, device_id_type=MESH,
+        ).start()
+        started["x"] += chips
+
+    across(z, chip)
+    wait(rows_all.at[pl.ds(0, len(side))], a_recv.at[z, 1])
     for c in near:
-        copy(xs(z, chip), xs(z, chip), x_recv.at[z, chip], on_chip(c))
-    reach = near[:2] if relay else near
-    for c in reach:
-        copy(a_ref, whole(z, chip), a_recv.at[z, chip, 0], on_chip(c))
-    for k in zs:
-        copy(a_ref, whole(z, chip), a_recv.at[z, chip, 0], {"dim": k})
-
-    def x_forward(plane):
-        wait(xs(plane, chip), x_recv.at[plane, chip])
-        for c in near:
-            copy(xs(plane, chip), xs(plane, chip), x_recv.at[plane, chip], on_chip(c))
-
-    def x_across(plane):
-        for c in near:
-            wait(xs(plane, c), x_recv.at[plane, c])
-        copy(xbuf.at[plane, core], xbuf.at[plane, core], xd_recv.at[plane], partner)
-
-    def a_forward(plane):
-        wait(whole(plane, chip), a_recv.at[plane, chip, 0])
-        for c in reach:
-            copy(whole(plane, chip), whole(plane, chip), a_recv.at[plane, chip, 0], on_chip(c))
-
-    def a_relay(plane):
-        for m, c in enumerate(reach):
-            wait(whole(plane, c), a_recv.at[plane, c, 0])
-            if relay:
-                copy(part(plane, c, m), part(plane, c, m), a_recv.at[plane, c, m], on_chip(near[1 - m]))
-
-    def a_across(plane):
-        if relay:
-            for h in range(2):
-                wait(part(plane, near[2], h), a_recv.at[plane, near[2], h])
-        copy(rows_all.at[plane, core], rows_all.at[plane, core], ad_recv.at[plane], partner)
-
+        across(z, c)
     for plane in zs:
-        x_forward(plane)
-    a_relay(z)
-    x_across(z)
+        across(plane, chip)
     for n, plane in enumerate(zs):
-        a_forward(plane)
-        if n == 0:
-            x_across(plane)
-            a_across(z)
-        else:
-            a_relay(zs[n - 1])
-            x_across(plane)
-            a_across(zs[n - 1])
-    if nz > 1:
-        a_relay(zs[-1])
-        a_across(zs[-1])
-
+        if square and n == 0:
+            wait(rows_all.at[slot(plane, diagonal)], a_recv.at[plane, 2])
+            across(plane, diagonal)
+        wait(rows_all.at[pl.ds(0, len(side))], a_recv.at[plane, 1])
+        for c in side:
+            across(plane, c)
+    if square:
+        for plane in zs[:0:-1]:
+            wait(rows_all.at[slot(plane, diagonal)], a_recv.at[plane, 2])
+            across(plane, diagonal)
+    planes = [z] + zs
     for plane in planes:
-        wait(xbuf.at[plane, 1 - core], xd_recv.at[plane])
+        wait(xbuf.at[pl.ds(slot(plane, 0, 1 - core), chips)], x_over.at[plane])
     eye = lax.broadcasted_iota(jnp.int32, (count, count), 1) == lax.broadcasted_iota(jnp.int32, (count, count), 0)
     for k in range(nz):
-        upd[2, k] = xbuf[k, :, :, :, 0:width].reshape(count, width)
+        upd[2, k] = xbuf[k * nd : (k + 1) * nd, :, 0:width].reshape(count, width)
 
     def piece_x():
         for k in range(nz):
@@ -194,27 +207,30 @@
     def row_sums(values):
         return jnp.sum(values, axis=1, keepdims=True)
 
-    marks = functools.reduce(jnp.add, [xbuf[k, :, :, :, width:].reshape(count, draws) for k in range(nz)])
-    targets = xbuf[0, :, :, :, width:].reshape(count, draws)
+    marks = functools.reduce(jnp.add, [xbuf[k * nd : (k + 1) * nd, :, width:].reshape(count, draws) for k in range(nz)])
+    targets = xbuf[0:nd, :, width:].reshape(count, draws)
     logits = jnp.concatenate([marks[g * rows : g * rows + 1] for g in range(nd)], axis=0)
     targets = jnp.concatenate([targets[g * rows + 1 : g * rows + 2] for g in range(nd)], axis=0)
     spread_at = lax.broadcasted_iota(jnp.int32, (count, LANES), 1) // per_row
     for plane in planes:
-        wait(rows_all.at[plane, 1 - core], ad_recv.at[plane])
+        wait(rows_all.at[pl.ds(slot(plane, 0, 1 - core), chips)], a_over.at[plane])
+
+    def basis(k):
+        return rows_all[k * nd : (k + 1) * nd].reshape(cols, width)
 
     def back(on_rows, on_x):
         left = halves(on_rows)
         left_x = halves(jnp.concatenate([on_x, on_x], axis=1))
         parts = []
         for k in range(nz):
-            product = dot(left, rows_all[k].reshape(cols, width))
+            product = dot(left, basis(k))
             product = product + dot(left_x, xpieces[:, k * width : (k + 1) * width])
             parts.append(fold(product))
         return parts
 
     def ahead(parts):
         pieces = [halves(v) for v in parts]
-        seen = functools.reduce(jnp.add, [dot_t(pieces[k], rows_all[k].reshape(cols, width)) for k in range(nz)])
+        seen = functools.reduce(jnp.add, [dot_t(pieces[k], basis(k)) for k in range(nz)])
         along = functools.reduce(
             jnp.add, [dot_t(pieces[k], xpieces[:, k * width : (k + 1) * width]) for k in range(nz)]
         )
@@ -281,8 +297,14 @@
         if not last:
             logits = logits + move_size * (on_drift * shift + on_image * shift_image)
         out_ref[t] = upd[t, z, pl.ds(pl.multiple_of((core * chips + chip) * rows, rows), rows), :]
-    for one in sent:
-        one.wait_send()
+    wait_sent(xbuf, "x", started["x"])
+    wait_sent(rows_all, "a", started["a"])
+    wait_sent(rows_all, "p", started["p"])
+    if square:
+
+        @pl.when(middle)
+        def _():
+            wait_sent(rows_all, "m", 2)
 
 
 def solution(mesh):
@@ -292,11 +314,6 @@
         rows, width = particles.shape
         draws = data_rows.shape[0] * data_rows.shape[1]
         count = nd * rows
-        chips = nd // 2
-        reach = 2 if chips == 4 else chips - 1
-        number = (chips - 1 + nz - 1) + (reach + nz - 1) + (nz - 1) * (chips - 1 + reach) + 2 * nz
-        if chips == 4:
-            number += 2 * nz
         dma = pltpu.SemaphoreType.DMA
         return pl.pallas_call(
             functools.partial(steps, nd, nz),
@@ -304,15 +321,15 @@
             in_specs=[pl.BlockSpec(memory_space=pltpu.VMEM)] * 3,
             out_specs=pl.BlockSpec(memory_space=pltpu.VMEM),
             scratch_shapes=[
-                pltpu.VMEM((nz, 2, chips, draws, width), bf16),
-                pltpu.VMEM((nz, 2, chips, rows, width + draws), f32),
+                pltpu.VMEM((nz * nd, draws, width), bf16),
+                pltpu.VMEM((nz * nd, rows, width + draws), f32),
                 pltpu.VMEM((2 * count, nz * width), bf16),
                 pltpu.VMEM((NEWTON + 1, nz, count, width), f32),
-                dma((nz, chips)),
+                dma((nz, 2)),
                 dma((nz,)),
-                dma((nz, chips, 2)),
+                dma((nz, 3)),
                 dma((nz,)),
-                dma((number,)),
+                dma((4,)),
             ],
             compiler_params=pltpu.CompilerParams(collective_id=0, has_side_effects=True),
         )(particles, data_rows.reshape(draws, width), labels)

time: 36.7 us -> 29.5 us (0.80)
  Pallas kernels: 35.1 us -> 27.9 us
    pallas_call x1, Pallas kernels: 35.1 us -> 27.9 us  [per_device(): pl.pallas_call(functools.partial(steps, nd, nz), out_shape=jax.ShapeDtype...]
where the time goes in v2:
time: 29.5 us; the launch traced here: 29.2 us
  Pallas kernels  27.9 us (95%)
  local copies, waits for them, and re-layouts  1.32 us (4%)
    pallas_call x1, Pallas kernels, per_device(): pl.pallas_call(functools.partial(steps, nd, nz), out_shape=jax.ShapeDtype...  27.9 us
    unnamed x1, local copies, waits for them, and re-layouts  1.32 us

profile of v2, /device:TPU:1, one launch (start us, length us, event | category | flops | bytes accessed | tf_op | source)
XLA Modules:
  0.0 29.2 jit_solution(7993980718646226514)
XLA Ops:
  0.0 27.9 %shard_map.37 = f32[2,8,256]{2,1,0:T(8,128)} custom-call(f32[8,256]{1,0:T(8,128)} %x_ref.1, bf16[128,256]{1,0:T(8,128)(2,1)} %bitcast.1, s32[8,16]{1,0:T(8,128)} %y_ref.1), custom_call_target="tpu_custom_call" | custom-call | tf_op jit(solution)/shard_map/pallas_call | solution.py:318
  27.9 1.3 %copy.5 = f32[2,8,256]{2,1,0:T(8,128)} copy(f32[2,8,256]{2,1,0:T(8,128)} %shard_map.37) | data formatting | bytes 32768

commit v3 on v2

v3 whole, which is shorter than its diff:
```python
import functools

import jax
import jax.numpy as jnp
from jax import lax
from jax.experimental import pallas as pl
from jax.experimental.pallas import tpu as pltpu
from jax.sharding import PartitionSpec as P

NEWTON = 2
BAND = 1
LANES = 128

prior_precision = 0.05
like_weight = 4.0
move_size = 0.5
MESH = pl.DeviceIdType.MESH
f32 = jnp.float32
bf16 = jnp.bfloat16


def halves(v):
    high = v.astype(bf16).astype(f32)
    return jnp.concatenate([high, v - high], axis=0).astype(bf16)


def fold(product):
    rows = product.shape[0] // 2
    return product[:rows] + product[rows:]


def paired(product):
    half = product.shape[1] // 2
    return product[:, :half] + product[:, half:]


def dot(a, b):
    return lax.dot_general(a, b, (((1,), (0,)), ((), ())), preferred_element_type=f32)


def dot_t(a, b):
    return lax.dot_general(a, b, (((1,), (1,)), ((), ())), preferred_element_type=f32)


def total_of(values):
    return jnp.sum(jnp.sum(values, axis=0, keepdims=True), axis=1, keepdims=True)


def steps(
    nd, nz, x_ref, a_ref, y_ref, out_ref,
    rows_all, turned, xbuf, xpieces, place, firsts,
    signs, x_recv, x_over, a_recv, a_over, send, load,
):
    rows, width = x_ref.shape
    draws = a_ref.shape[0]
    per_row = draws // rows
    chips = nd // 2
    slots = nz * nd
    count = nd * rows
    cols = nd * draws
    scale = 1.0 * BAND * width * nz
    cross = 4.0 / (scale * scale)
    me_dom = lax.axis_index("dom")
    z = lax.axis_index("dim")
    chip, core = me_dom // 2, me_dom % 2
    square = chips == 4 and nz == 4

    if square:
        near = [chip + 1 - 2 * (chip % 2), chip + 2 - 4 * (chip // 2), 3 - chip]
        high = z // 2
        middle = (z + 1) // 2 % 2 == 1
        zs = [3 - 3 * high, 2 - high, z + 1 - 2 * (z % 2)]
    else:
        near = [(chip + m) % chips for m in range(1, chips)]
        zs = [(z + k) % nz for k in range(1, nz)]
    partner = {"dom": me_dom + 1 - 2 * core}
    started = {"x": 0, "a": 0, "p": 0}
    sems = {"x": send.at[0], "a": send.at[1], "p": send.at[2], "m": send.at[3]}

    def on_chip(c):
        return {"dom": c * 2 + core}

    def slot(plane, c, k=None):
        return (plane * 2 + (core if k is None else k)) * chips + c

    def copy(kind, ref, recv, device):
        pltpu.make_async_remote_copy(
            src_ref=ref, dst_ref=ref, send_sem=sems[kind], recv_sem=recv,
            device_id=device, device_id_type=MESH,
        ).start()
        if kind in started:
            started[kind] += 1

    def wait(ref, recv):
        pltpu.make_async_remote_copy(
            src_ref=ref, dst_ref=ref, send_sem=send.at[0], recv_sem=recv, device_id=partner, device_id_type=MESH,
        ).wait_recv()

    def wait_sent(ref, kind, number):
        while number > 0:
            part = ref.at[pl.ds(0, min(number, slots))]
            pltpu.make_async_remote_copy(
                src_ref=part, dst_ref=part, send_sem=sems[kind], recv_sem=send.at[0],
                device_id=partner, device_id_type=MESH,
            ).wait_send()
            number -= slots

    barrier = pltpu.get_barrier_semaphore()
    greet = [on_chip(c) for c in near] + [{"dim": k} for k in zs] + [partner]
    for device in greet:
        pl.semaphore_signal(barrier, inc=1, device_id=device, device_id_type=MESH)

    here = slot(z, chip)
    loads = [
        pltpu.make_async_copy(x_ref, xbuf.at[here, :, pl.ds(0, width)], load.at[0]),
        pltpu.make_async_copy(a_ref, rows_all.at[here], load.at[1]),
        pltpu.make_async_copy(y_ref, signs, load.at[2]),
    ]
    for one in loads:
        one.start()
    lane_of = lax.broadcasted_iota(jnp.int32, (rows, draws), 1) // per_row
    row_of = lax.broadcasted_iota(jnp.int32, (rows, draws), 0)
    own_block = lane_of == row_of

    def flat(values):
        return jnp.sum(jnp.where(own_block, values, 0.0), axis=0, keepdims=True)

    tile = lax.broadcasted_iota(jnp.int32, (per_row, draws), 1) % per_row
    tile = (tile == lax.broadcasted_iota(jnp.int32, (per_row, draws), 0)).astype(f32).astype(bf16)
    for one in loads:
        one.wait()
    labels = flat(dot(signs[...].astype(f32).astype(bf16), tile))
    first = flat(fold(dot_t(halves(xbuf[here, :, 0:width]), rows_all[here])))
    xbuf[here, :, width:] = jnp.concatenate([first, labels, jnp.zeros((rows - 2, draws), f32)], axis=0)
    pl.semaphore_wait(barrier, len(greet))

    def send_x(plane, devices, role):
        for device in devices:
            copy("x", xbuf.at[slot(plane, chip)], x_recv.at[plane, role], device)

    def send_a(plane, devices, role):
        for device in devices:
            copy("a", rows_all.at[slot(plane, chip)], a_recv.at[plane, role], device)

    plane_devices = [on_chip(c) for c in near]
    z_devices = [{"dim": k} for k in zs]
    side, diagonal = (near[:2], near[2]) if square else (near, None)
    send_x(z, z_devices, 0)
    send_x(z, plane_devices, 1)
    send_a(z, plane_devices[: len(side)], 1)
    if square:
        send_a(z, plane_devices[2:], 2)
    send_a(z, z_devices, 0)
    for plane in zs:
        wait(xbuf.at[slot(plane, chip)], x_recv.at[plane, 0])
        send_x(plane, plane_devices, 1)

    def across(plane, c):
        copy("p", rows_all.at[slot(plane, c)], a_over.at[plane], partner)

    for n, plane in enumerate(zs):
        wait(rows_all.at[slot(plane, chip)], a_recv.at[plane, 0])
        if square and n == 0:
            send_a(plane, plane_devices[2:], 2)
        send_a(plane, plane_devices[: len(side)], 1)
        if square and n == 0:
            from_corner = rows_all.at[slot(z, diagonal)]
            wait(from_corner, a_recv.at[z, 2])
            copy("a", from_corner, a_recv.at[z, 2], z_devices[2])

            @pl.when(middle)
            def _():
                for device in z_devices[:2]:
                    copy("m", from_corner, a_recv.at[z, 2], device)

    for plane in [z] + zs:
        wait(xbuf.at[pl.ds(0, len(near))], x_recv.at[plane, 1])
        bundle = xbuf.at[pl.ds(slot(plane, 0), chips)]
        pltpu.make_async_remote_copy(
            src_ref=bundle, dst_ref=bundle, send_sem=sems["x"], recv_sem=x_over.at[plane],
            device_id=partner, device_id_type=MESH,
        ).start()
        started["x"] += chips

    across(z, chip)
    wait(rows_all.at[pl.ds(0, len(side))], a_recv.at[z, 1])
    for c in near:
        across(z, c)
    for plane in zs:
        across(plane, chip)
    planes = [z] + zs
    for plane in planes:
        wait(xbuf.at[pl.ds(slot(plane, 0, 1 - core), chips)], x_over.at[plane])
    eye = lax.broadcasted_iota(jnp.int32, (count, count), 1) == lax.broadcasted_iota(jnp.int32, (count, count), 0)
    spread_at = lax.broadcasted_iota(jnp.int32, (count, LANES), 1) // per_row
    for k in range(nz):
        place[k] = xbuf[k * nd : (k + 1) * nd, :, 0:width].reshape(count, width)

    def row_sums(values):
        return jnp.sum(values, axis=1, keepdims=True)

    marks = functools.reduce(jnp.add, [xbuf[k * nd : (k + 1) * nd, :, width:].reshape(count, draws) for k in range(nz)])
    targets = xbuf[0:nd, :, width:].reshape(count, draws)
    logits = jnp.concatenate([marks[g * rows : g * rows + 1] for g in range(nd)], axis=0)
    targets = jnp.concatenate([targets[g * rows + 1 : g * rows + 2] for g in range(nd)], axis=0)

    def prepare(logits):
        for k in range(nz):
            xpieces[k] = halves(place[k])
        inner = paired(fold(functools.reduce(jnp.add, [dot_t(xpieces[k], xpieces[k]) for k in range(nz)])))
        diagonal = jnp.where(eye, inner, 0.0)
        distance = row_sums(diagonal) + jnp.sum(diagonal, axis=0, keepdims=True) - 2.0 * inner
        kernel = jnp.exp(distance * (-1.0 / scale))
        prob = 1.0 / (1.0 + jnp.exp(-logits))
        curve = like_weight * prob * (1.0 - prob)
        gap = like_weight * (targets - prob)
        kernel_sq = kernel * kernel
        padded = kernel
        if count < LANES:
            padded = jnp.concatenate([kernel, jnp.zeros((count, LANES - count), f32)], axis=1)
        drive, weight = [], []
        for g in range(nd):
            at = g * rows
            block = padded[:, at // LANES * LANES : at // LANES * LANES + LANES]
            wide = jnp.take_along_axis(block, spread_at + at % LANES, axis=1)
            drive.append(wide * gap[g : g + 1])
            weight.append(wide * wide * curve[g : g + 1])
        pull = (-prior_precision - 2.0 / scale) * kernel + jnp.where(eye, (2.0 / scale) * row_sums(kernel), 0.0)
        drive, weight = jnp.concatenate(drive, axis=1), jnp.concatenate(weight, axis=1)
        return kernel_sq, row_sums(kernel_sq), weight, drive, pull

    def basis(k):
        return rows_all[pl.ds(k * nd, nd)].reshape(cols, width)

    def lefts(on_rows, on_x):
        return halves(on_rows), halves(jnp.concatenate([on_x, on_x], axis=1))

    def back(left, left_x, k):
        return fold(dot(left, basis(k)) + dot(left_x, xpieces[k]))

    def ahead(parts):
        pieces = [halves(v) for v in parts]
        seen = dot(jnp.concatenate(pieces, axis=1), turned[...])
        along = functools.reduce(jnp.add, [dot_t(pieces[k], xpieces[k]) for k in range(nz)])
        return fold(seen), paired(fold(along))

    def own_logits(seen):
        return jnp.concatenate(
            [flat(seen[g * rows : (g + 1) * rows, g * draws : (g + 1) * draws]) for g in range(nd)], axis=0
        )

    kernel_sq, total_sq, weight, drive, pull = prepare(logits)
    left, left_x = lefts(drive, pull)

    def begin(plane):
        wait(rows_all.at[pl.ds(slot(plane, 0, 1 - core), chips)], a_over.at[plane])
        part = back(left, left_x, plane) / count
        firsts[plane] = part
        pieces = halves(part)
        turned[pl.ds(pl.multiple_of(plane * width, width), width), :] = basis(plane).T
        return dot_t(pieces, basis(plane)), dot_t(pieces, xpieces[plane])

    started_parts = [begin(z)]
    for n, plane in enumerate(zs):
        if square and n == 0:
            wait(rows_all.at[slot(plane, diagonal)], a_recv.at[plane, 2])
            across(plane, diagonal)
        wait(rows_all.at[pl.ds(0, len(side))], a_recv.at[plane, 1])
        for c in side:
            across(plane, c)
    if square:
        for plane in zs[:0:-1]:
            wait(rows_all.at[slot(plane, diagonal)], a_recv.at[plane, 2])
            across(plane, diagonal)
    started_parts += [begin(plane) for plane in zs]
    seen = fold(functools.reduce(jnp.add, [part[0] for part in started_parts]))
    along = paired(fold(functools.reduce(jnp.add, [part[1] for part in started_parts])))
    drift = [firsts[k] for k in range(nz)]

    for t in range(NEWTON):
        last = t + 1 == NEWTON
        if t > 0:
            kernel_sq, total_sq, weight, drive, pull = prepare(logits)
            left, left_x = lefts(drive, pull)
            drift = [back(left, left_x, k) / count for k in range(nz)]
            seen, along = ahead(drift)
        shift = own_logits(seen)
        on_x = cross * kernel_sq * (along - row_sums(jnp.where(eye, along, 0.0)))
        on_x = on_x - jnp.where(eye, row_sums(on_x), 0.0)
        left, left_x = lefts(weight * seen, on_x)
        image = [(back(left, left_x, k) + prior_precision * total_sq * drift[k]) / count for k in range(nz)]
        seen, along = ahead(image)
        shift_image = own_logits(seen)
        along = along - row_sums(jnp.where(eye, along, 0.0))
        norm = total_of(functools.reduce(jnp.add, [d * d for d in drift]))
        curve_total = total_of(functools.reduce(jnp.add, [d * v for d, v in zip(drift, image)]))
        squares = functools.reduce(jnp.add, [v * v for v in image])
        image_square = total_of(squares)
        bent = total_of(prior_precision * total_sq * row_sums(squares) + cross * row_sums(kernel_sq * along * along))
        bent = (bent + total_of(weight * seen * seen)) / count
        alpha = norm / curve_total
        norm_next = norm - 2.0 * alpha * curve_total + alpha * alpha * image_square
        keep = 1.0 + norm_next / norm
        curve_next = keep * keep * curve_total - 2.0 * keep * alpha * image_square + alpha * alpha * bent
        alpha_next = norm_next / curve_next
        on_drift, on_image = alpha + alpha_next * keep, -alpha_next * alpha
        for k in range(nz):
            firsts[k] = on_drift * drift[k] + on_image * image[k]
        out_ref[t] = firsts[z, pl.ds(pl.multiple_of((core * chips + chip) * rows, rows), rows), :]
        if not last:
            for k in range(nz):
                place[k] = place[k] + move_size * firsts[k]
            logits = logits + move_size * (on_drift * shift + on_image * shift_image)
    wait_sent(xbuf, "x", started["x"])
    wait_sent(rows_all, "a", started["a"])
    wait_sent(rows_all, "p", started["p"])
    if square:

        @pl.when(middle)
        def _():
            wait_sent(rows_all, "m", 2)


def solution(mesh):
    nd, nz = mesh.shape["dom"], mesh.shape["dim"]

    def per_device(particles, data_rows, labels):
        rows, width = particles.shape
        draws = data_rows.shape[0] * data_rows.shape[1]
        count = nd * rows
        dma = pltpu.SemaphoreType.DMA
        return pl.pallas_call(
            functools.partial(steps, nd, nz),
            out_shape=pltpu.VMEM((NEWTON, rows, width), f32),
            in_specs=[pl.BlockSpec(memory_space=pl.ANY)] * 3,
            out_specs=pl.BlockSpec(memory_space=pltpu.VMEM),
            scratch_shapes=[
                pltpu.VMEM((nz * nd, draws, width), bf16),
                pltpu.VMEM((nz * width, nd * draws), bf16),
                pltpu.VMEM((nz * nd, rows, width + draws), f32),
                pltpu.VMEM((nz, 2 * count, width), bf16),
                pltpu.VMEM((nz, count, width), f32),
                pltpu.VMEM((nz, count, width), f32),
                pltpu.VMEM(labels.shape, jnp.int32),
                dma((nz, 2)),
                dma((nz,)),
                dma((nz, 3)),
                dma((nz,)),
                dma((4,)),
                dma((3,)),
            ],
            compiler_params=pltpu.CompilerParams(collective_id=0, has_side_effects=True, vmem_limit_bytes=67_000_000),
        )(particles, data_rows.reshape(draws, width), labels)

    placed = (P("dom", "dim"), P("dom", None, "dim"), P("dom", None))
    return jax.shard_map(
        per_device, mesh=mesh, in_specs=placed, out_specs=P(None, "dom", "dim"), check_vma=False
    )
```

time: 29.5 us -> 25.8 us (0.87)
  Pallas kernels: 27.9 us -> 25 us
  local copies, waits for them, and re-layouts: 1.32 us -> 0.61 us
    pallas_call x1, Pallas kernels: 27.9 us -> 25 us  [per_device(): pl.pallas_call(functools.partial(steps, nd, nz), out_shape=pltpu.VMEM((NE...]
    unnamed x1, local copies, waits for them, and re-layouts: 1.32 us -> 0.61 us
where the time goes in v3:
time: 25.8 us; the launch traced here: 25.6 us
  Pallas kernels  25 us (97%)
  local copies, waits for them, and re-layouts  0.61 us (2%)
    pallas_call x1, Pallas kernels, per_device(): pl.pallas_call(functools.partial(steps, nd, nz), out_shape=pltpu.VMEM((NE...  25 us
    unnamed x1, local copies, waits for them, and re-layouts  0.61 us

profile of v3, /device:TPU:1, one launch (start us, length us, event | category | flops | bytes accessed | tf_op | source)
XLA Modules:
  0.0 25.6 jit_solution(8646841609522687561)
XLA Ops:
  0.0 25.0 %shard_map.37 = f32[2,8,256]{2,1,0:T(8,128)S(1)} custom-call(f32[8,256]{1,0:T(8,128)} %x_ref.1, bf16[128,256]{1,0:T(8,128)(2,1)} %bitcast.1, s32[8,16]{1,0:T(8,128)} %y_ref.1), custom_call_target="tpu_custom_call" | custom-call | tf_op jit(solution)/shard_map/pallas_call | solution.py:332
  25.0 0.6 %copy.5 = f32[2,8,256]{2,1,0:T(8,128)} copy(f32[2,8,256]{2,1,0:T(8,128)S(1)} %shard_map.37) | data formatting | bytes 32768

commit v4 on v3

--- a/solution.py
+++ b/solution.py
@@ -58,6 +58,8 @@
     slots = nz * nd
     count = nd * rows
     cols = nd * draws
+    blocks = width // LANES
+    message = blocks * rows + 2
     scale = 1.0 * BAND * width * nz
     cross = 4.0 / (scale * scale)
     me_dom = lax.axis_index("dom")
@@ -98,7 +100,7 @@
 
     def wait_sent(ref, kind, number):
         while number > 0:
-            part = ref.at[pl.ds(0, min(number, slots))]
+            part = ref(min(number, slots))
             pltpu.make_async_remote_copy(
                 src_ref=part, dst_ref=part, send_sem=sems[kind], recv_sem=send.at[0],
                 device_id=partner, device_id_type=MESH,
@@ -112,10 +114,13 @@
 
     here = slot(z, chip)
     loads = [
-        pltpu.make_async_copy(x_ref, xbuf.at[here, :, pl.ds(0, width)], load.at[0]),
-        pltpu.make_async_copy(a_ref, rows_all.at[here], load.at[1]),
-        pltpu.make_async_copy(y_ref, signs, load.at[2]),
+        pltpu.make_async_copy(
+            x_ref.at[:, pl.ds(b * LANES, LANES)], xbuf.at[here, pl.ds(b * rows, rows), :], load.at[2 + b]
+        )
+        for b in range(blocks)
     ]
+    loads.append(pltpu.make_async_copy(a_ref, rows_all.at[here], load.at[0]))
+    loads.append(pltpu.make_async_copy(y_ref, signs, load.at[1]))
     for one in loads:
         one.start()
     lane_of = lax.broadcasted_iota(jnp.int32, (rows, draws), 1) // per_row
@@ -130,13 +135,17 @@
     for one in loads:
         one.wait()
     labels = flat(dot(signs[...].astype(f32).astype(bf16), tile))
-    first = flat(fold(dot_t(halves(xbuf[here, :, 0:width]), rows_all[here])))
-    xbuf[here, :, width:] = jnp.concatenate([first, labels, jnp.zeros((rows - 2, draws), f32)], axis=0)
+    own_x = jnp.concatenate([xbuf[here, b * rows : (b + 1) * rows, :] for b in range(blocks)], axis=1)
+    first = flat(fold(dot_t(halves(own_x), rows_all[here])))
+    xbuf[here, blocks * rows : blocks * rows + 2, :] = jnp.concatenate([first, labels], axis=0)
     pl.semaphore_wait(barrier, len(greet))
+
+    def xs(at, number=None):
+        return xbuf.at[at if number is None else pl.ds(at, number), pl.ds(0, message), :]
 
     def send_x(plane, devices, role):
         for device in devices:
-            copy("x", xbuf.at[slot(plane, chip)], x_recv.at[plane, role], device)
+            copy("x", xs(slot(plane, chip)), x_recv.at[plane, role], device)
 
     def send_a(plane, devices, role):
         for device in devices:
@@ -147,12 +156,12 @@
     side, diagonal = (near[:2], near[2]) if square else (near, None)
     send_x(z, z_devices, 0)
     send_x(z, plane_devices, 1)
-    send_a(z, plane_devices[: len(side)], 1)
     if square:
         send_a(z, plane_devices[2:], 2)
+    send_a(z, plane_devices[: len(side)], 1)
     send_a(z, z_devices, 0)
     for plane in zs:
-        wait(xbuf.at[slot(plane, chip)], x_recv.at[plane, 0])
+        wait(xs(slot(plane, chip)), x_recv.at[plane, 0])
         send_x(plane, plane_devices, 1)
 
     def across(plane, c):
@@ -174,8 +183,8 @@
                     copy("m", from_corner, a_recv.at[z, 2], device)
 
     for plane in [z] + zs:
-        wait(xbuf.at[pl.ds(0, len(near))], x_recv.at[plane, 1])
-        bundle = xbuf.at[pl.ds(slot(plane, 0), chips)]
+        wait(xs(0, len(near)), x_recv.at[plane, 1])
+        bundle = xs(slot(plane, 0), chips)
         pltpu.make_async_remote_copy(
             src_ref=bundle, dst_ref=bundle, send_sem=sems["x"], recv_sem=x_over.at[plane],
             device_id=partner, device_id_type=MESH,
@@ -188,21 +197,10 @@
         across(z, c)
     for plane in zs:
         across(plane, chip)
-    planes = [z] + zs
-    for plane in planes:
-        wait(xbuf.at[pl.ds(slot(plane, 0, 1 - core), chips)], x_over.at[plane])
     eye = lax.broadcasted_iota(jnp.int32, (count, count), 1) == lax.broadcasted_iota(jnp.int32, (count, count), 0)
     spread_at = lax.broadcasted_iota(jnp.int32, (count, LANES), 1) // per_row
-    for k in range(nz):
-        place[k] = xbuf[k * nd : (k + 1) * nd, :, 0:width].reshape(count, width)
-
     def row_sums(values):
         return jnp.sum(values, axis=1, keepdims=True)
-
-    marks = functools.reduce(jnp.add, [xbuf[k * nd : (k + 1) * nd, :, width:].reshape(count, draws) for k in range(nz)])
-    targets = xbuf[0:nd, :, width:].reshape(count, draws)
-    logits = jnp.concatenate([marks[g * rows : g * rows + 1] for g in range(nd)], axis=0)
-    targets = jnp.concatenate([targets[g * rows + 1 : g * rows + 2] for g in range(nd)], axis=0)
 
     def prepare(logits):
         for k in range(nz):
@@ -232,63 +230,88 @@
     def basis(k):
         return rows_all[pl.ds(k * nd, nd)].reshape(cols, width)
 
-    def lefts(on_rows, on_x):
-        return halves(on_rows), halves(jnp.concatenate([on_x, on_x], axis=1))
-
-    def back(left, left_x, k):
-        return fold(dot(left, basis(k)) + dot(left_x, xpieces[k]))
-
     def ahead(parts):
-        pieces = [halves(v) for v in parts]
-        seen = dot(jnp.concatenate(pieces, axis=1), turned[...])
-        along = functools.reduce(jnp.add, [dot_t(pieces[k], xpieces[k]) for k in range(nz)])
-        return fold(seen), paired(fold(along))
+        seen = dot(jnp.concatenate([halves(v) for v in parts], axis=1), turned[...])
+        along = functools.reduce(jnp.add, [dot_t(parts[k].astype(bf16), xpieces[k, 0:count]) for k in range(nz)])
+        return fold(seen), along
 
     def own_logits(seen):
         return jnp.concatenate(
             [flat(seen[g * rows : (g + 1) * rows, g * draws : (g + 1) * draws]) for g in range(nd)], axis=0
         )
 
-    kernel_sq, total_sq, weight, drive, pull = prepare(logits)
-    left, left_x = lefts(drive, pull)
-
-    def begin(plane):
-        wait(rows_all.at[pl.ds(slot(plane, 0, 1 - core), chips)], a_over.at[plane])
-        part = back(left, left_x, plane) / count
-        firsts[plane] = part
-        pieces = halves(part)
-        turned[pl.ds(pl.multiple_of(plane * width, width), width), :] = basis(plane).T
-        return dot_t(pieces, basis(plane)), dot_t(pieces, xpieces[plane])
-
-    started_parts = [begin(z)]
-    for n, plane in enumerate(zs):
+
+    def hand_over(n):
+        plane = zs[n]
         if square and n == 0:
             wait(rows_all.at[slot(plane, diagonal)], a_recv.at[plane, 2])
             across(plane, diagonal)
         wait(rows_all.at[pl.ds(0, len(side))], a_recv.at[plane, 1])
         for c in side:
             across(plane, c)
-    if square:
-        for plane in zs[:0:-1]:
-            wait(rows_all.at[slot(plane, diagonal)], a_recv.at[plane, 2])
-            across(plane, diagonal)
+
+    def hand_corners():
+        if square:
+            for plane in zs[:0:-1]:
+                wait(rows_all.at[slot(plane, diagonal)], a_recv.at[plane, 2])
+                across(plane, diagonal)
+
+    if len(zs) > 0:
+        hand_over(0)
+    planes = [z] + zs
+    for plane in planes:
+        wait(xs(slot(plane, 0, 1 - core), chips), x_over.at[plane])
+    for k in range(nz):
+        for b in range(blocks):
+            block = xbuf[k * nd : (k + 1) * nd, b * rows : (b + 1) * rows, :].reshape(count, LANES)
+            place[k, :, b * LANES : (b + 1) * LANES] = block
+
+    def messages(k, row):
+        return jnp.concatenate([xbuf[k * nd + g, row : row + 1, :] for g in range(nd)], axis=0)
+
+    logits = functools.reduce(jnp.add, [messages(k, blocks * rows) for k in range(nz)])
+    targets = messages(0, blocks * rows + 1)
+
+    kernel_sq, total_sq, weight, drive, pull = prepare(logits)
+    left = halves(drive)
+    left_x = halves(jnp.concatenate([pull, pull], axis=1))
+
+    def begin(plane):
+        wait(rows_all.at[pl.ds(slot(plane, 0, 1 - core), chips)], a_over.at[plane])
+        rows_here = basis(plane)
+        part = fold(dot(left, rows_here) + dot(left_x, xpieces[plane])) / count
+        firsts[plane] = part
+        turned[pl.ds(pl.multiple_of(plane * width, width), width), :] = rows_here.T
+        return dot_t(halves(part), rows_here), dot_t(part.astype(bf16), xpieces[plane, 0:count])
+
+    started_parts = [begin(z)]
+    if len(zs) > 1:
+        hand_over(1)
+    if len(zs) > 2:
+        hand_over(2)
+    hand_corners()
     started_parts += [begin(plane) for plane in zs]
     seen = fold(functools.reduce(jnp.add, [part[0] for part in started_parts]))
-    along = paired(fold(functools.reduce(jnp.add, [part[1] for part in started_parts])))
+    along = functools.reduce(jnp.add, [part[1] for part in started_parts])
     drift = [firsts[k] for k in range(nz)]
 
     for t in range(NEWTON):
         last = t + 1 == NEWTON
         if t > 0:
             kernel_sq, total_sq, weight, drive, pull = prepare(logits)
-            left, left_x = lefts(drive, pull)
-            drift = [back(left, left_x, k) / count for k in range(nz)]
+            left = halves(drive)
+            left_x = halves(jnp.concatenate([pull, pull], axis=1))
+            drift = [fold(dot(left, basis(k)) + dot(left_x, xpieces[k])) / count for k in range(nz)]
             seen, along = ahead(drift)
         shift = own_logits(seen)
         on_x = cross * kernel_sq * (along - row_sums(jnp.where(eye, along, 0.0)))
         on_x = on_x - jnp.where(eye, row_sums(on_x), 0.0)
-        left, left_x = lefts(weight * seen, on_x)
-        image = [(back(left, left_x, k) + prior_precision * total_sq * drift[k]) / count for k in range(nz)]
+        left, left_x = halves(weight * seen), on_x.astype(bf16)
+        image = [
+            (fold(dot(left, basis(k))) + dot(left_x, xpieces[k, 0:count]) + prior_precision * total_sq * drift[k])
+            / count
+            for k in range(nz)
+        ]
         seen, along = ahead(image)
         shift_image = own_logits(seen)
         along = along - row_sums(jnp.where(eye, along, 0.0))
@@ -311,14 +334,14 @@
             for k in range(nz):
                 place[k] = place[k] + move_size * firsts[k]
             logits = logits + move_size * (on_drift * shift + on_image * shift_image)
-    wait_sent(xbuf, "x", started["x"])
-    wait_sent(rows_all, "a", started["a"])
-    wait_sent(rows_all, "p", started["p"])
+    wait_sent(lambda number: xs(0, number), "x", started["x"])
+    wait_sent(lambda number: rows_all.at[pl.ds(0, number)], "a", started["a"])
+    wait_sent(lambda number: rows_all.at[pl.ds(0, number)], "p", started["p"])
     if square:
 
         @pl.when(middle)
         def _():
-            wait_sent(rows_all, "m", 2)
+            wait_sent(lambda number: rows_all.at[pl.ds(0, number)], "m", 2)
 
 
 def solution(mesh):
@@ -337,7 +360,7 @@
             scratch_shapes=[
                 pltpu.VMEM((nz * nd, draws, width), bf16),
                 pltpu.VMEM((nz * width, nd * draws), bf16),
-                pltpu.VMEM((nz * nd, rows, width + draws), f32),
+                pltpu.VMEM((nz * nd, -(-(width // LANES * rows + 2) // 8) * 8, LANES), f32),
                 pltpu.VMEM((nz, 2 * count, width), bf16),
                 pltpu.VMEM((nz, count, width), f32),
                 pltpu.VMEM((nz, count, width), f32),
@@ -347,7 +370,7 @@
                 dma((nz, 3)),
                 dma((nz,)),
                 dma((4,)),
-                dma((3,)),
+                dma((2 + width // LANES,)),
             ],
             compiler_params=pltpu.CompilerParams(collective_id=0, has_side_effects=True, vmem_limit_bytes=67_000_000),
         )(particles, data_rows.reshape(draws, width), labels)

time: 25.8 us -> 24.4 us (0.946)
  Pallas kernels: 25 us -> 23.6 us
    pallas_call x1, Pallas kernels: 25 us -> 23.6 us  [per_device(): pl.pallas_call(functools.partial(steps, nd, nz), out_shape=pltpu.VMEM((NE...]
where the time goes in v4:
time: 24.4 us; the launch traced here: 24.2 us
  Pallas kernels  23.6 us (97%)
  local copies, waits for them, and re-layouts  0.61 us (2%)
    pallas_call x1, Pallas kernels, per_device(): pl.pallas_call(functools.partial(steps, nd, nz), out_shape=pltpu.VMEM((NE...  23.6 us
    unnamed x1, local copies, waits for them, and re-layouts  0.61 us

profile of v4, /device:TPU:1, one launch (start us, length us, event | category | flops | bytes accessed | tf_op | source)
XLA Modules:
  0.0 24.2 jit_solution(7308606034730312833)
XLA Ops:
  0.0 23.6 %shard_map.37 = f32[2,8,256]{2,1,0:T(8,128)S(1)} custom-call(f32[8,256]{1,0:T(8,128)} %x_ref.1, bf16[128,256]{1,0:T(8,128)(2,1)} %bitcast.1, s32[8,16]{1,0:T(8,128)} %y_ref.1), custom_call_target="tpu_custom_call" | custom-call | tf_op jit(solution)/shard_map/pallas_call | solution.py:355
  23.6 0.6 %copy.5 = f32[2,8,256]{2,1,0:T(8,128)} copy(f32[2,8,256]{2,1,0:T(8,128)S(1)} %shard_map.37) | data formatting | bytes 32768

commit v5 on v4

--- a/solution.py
+++ b/solution.py
@@ -48,7 +48,7 @@
 
 def steps(
     nd, nz, x_ref, a_ref, y_ref, out_ref,
-    rows_all, turned, xbuf, xpieces, place, firsts,
+    rows_all, turned, xbuf, xpieces, place, firsts, seconds,
     signs, x_recv, x_over, a_recv, a_over, send, load,
 ):
     rows, width = x_ref.shape
@@ -76,8 +76,8 @@
         near = [(chip + m) % chips for m in range(1, chips)]
         zs = [(z + k) % nz for k in range(1, nz)]
     partner = {"dom": me_dom + 1 - 2 * core}
-    started = {"x": 0, "a": 0, "p": 0}
-    sems = {"x": send.at[0], "a": send.at[1], "p": send.at[2], "m": send.at[3]}
+    started = {"x": 0, "a": 0}
+    sems = {"x": send.at[0], "a": send.at[1], "m": send.at[1]}
 
     def on_chip(c):
         return {"dom": c * 2 + core}
@@ -115,7 +115,7 @@
     here = slot(z, chip)
     loads = [
         pltpu.make_async_copy(
-            x_ref.at[:, pl.ds(b * LANES, LANES)], xbuf.at[here, pl.ds(b * rows, rows), :], load.at[2 + b]
+            x_ref.at[:, pl.ds(b * LANES, LANES)], xbuf.at[here, pl.ds(b * rows, rows), :], load.at[2]
         )
         for b in range(blocks)
     ]
@@ -132,7 +132,9 @@
 
     tile = lax.broadcasted_iota(jnp.int32, (per_row, draws), 1) % per_row
     tile = (tile == lax.broadcasted_iota(jnp.int32, (per_row, draws), 0)).astype(f32).astype(bf16)
-    for one in loads:
+    own_places = xbuf.at[here, pl.ds(0, blocks * rows), :]
+    pltpu.make_async_copy(own_places, own_places, load.at[2]).wait()
+    for one in loads[blocks:]:
         one.wait()
     labels = flat(dot(signs[...].astype(f32).astype(bf16), tile))
     own_x = jnp.concatenate([xbuf[here, b * rows : (b + 1) * rows, :] for b in range(blocks)], axis=1)
@@ -143,9 +145,9 @@
     def xs(at, number=None):
         return xbuf.at[at if number is None else pl.ds(at, number), pl.ds(0, message), :]
 
-    def send_x(plane, devices, role):
+    def send_x(plane, devices, recv):
         for device in devices:
-            copy("x", xs(slot(plane, chip)), x_recv.at[plane, role], device)
+            copy("x", xs(slot(plane, chip)), x_recv.at[recv], device)
 
     def send_a(plane, devices, role):
         for device in devices:
@@ -154,18 +156,19 @@
     plane_devices = [on_chip(c) for c in near]
     z_devices = [{"dim": k} for k in zs]
     side, diagonal = (near[:2], near[2]) if square else (near, None)
-    send_x(z, z_devices, 0)
-    send_x(z, plane_devices, 1)
+    corner_first = plane_devices[len(side) :] + plane_devices[: len(side)]
+    send_x(z, z_devices, z)
+    send_x(z, corner_first, nz)
     if square:
         send_a(z, plane_devices[2:], 2)
     send_a(z, plane_devices[: len(side)], 1)
     send_a(z, z_devices, 0)
     for plane in zs:
-        wait(xs(slot(plane, chip)), x_recv.at[plane, 0])
-        send_x(plane, plane_devices, 1)
+        wait(xs(slot(plane, chip)), x_recv.at[plane])
+        send_x(plane, corner_first, nz)
 
     def across(plane, c):
-        copy("p", rows_all.at[slot(plane, c)], a_over.at[plane], partner)
+        copy("a", rows_all.at[slot(plane, c)], a_over.at[plane], partner)
 
     for n, plane in enumerate(zs):
         wait(rows_all.at[slot(plane, chip)], a_recv.at[plane, 0])
@@ -182,14 +185,10 @@
                 for device in z_devices[:2]:
                     copy("m", from_corner, a_recv.at[z, 2], device)
 
+    wait(xs(0, nz * len(near)), x_recv.at[nz])
     for plane in [z] + zs:
-        wait(xs(0, len(near)), x_recv.at[plane, 1])
-        bundle = xs(slot(plane, 0), chips)
-        pltpu.make_async_remote_copy(
-            src_ref=bundle, dst_ref=bundle, send_sem=sems["x"], recv_sem=x_over.at[plane],
-            device_id=partner, device_id_type=MESH,
-        ).start()
-        started["x"] += chips
+        copy("x", xs(slot(plane, 0), chips), x_over.at[0], partner)
+        started["x"] += chips - 1
 
     across(z, chip)
     wait(rows_all.at[pl.ds(0, len(side))], a_recv.at[z, 1])
@@ -259,8 +258,7 @@
     if len(zs) > 0:
         hand_over(0)
     planes = [z] + zs
-    for plane in planes:
-        wait(xs(slot(plane, 0, 1 - core), chips), x_over.at[plane])
+    wait(xs(0, nz * chips), x_over.at[0])
     for k in range(nz):
         for b in range(blocks):
             block = xbuf[k * nd : (k + 1) * nd, b * rows : (b + 1) * rows, :].reshape(count, LANES)
@@ -276,23 +274,31 @@
     left = halves(drive)
     left_x = halves(jnp.concatenate([pull, pull], axis=1))
 
-    def begin(plane):
+    def begin(group):
+        on_rows, on_places = [], []
+        for plane in group:
+            rows_here = basis(plane)
+            part = fold(dot(left, rows_here) + dot(left_x, xpieces[plane])) / count
+            firsts[plane] = part
+            turned[pl.ds(pl.multiple_of(plane * width, width), width), :] = rows_here.T
+            on_rows.append(dot_t(halves(part), rows_here))
+            on_places.append(dot_t(part.astype(bf16), xpieces[plane, 0:count]))
+        return fold(functools.reduce(jnp.add, on_rows)), functools.reduce(jnp.add, on_places)
+
+    def landed(plane):
         wait(rows_all.at[pl.ds(slot(plane, 0, 1 - core), chips)], a_over.at[plane])
-        rows_here = basis(plane)
-        part = fold(dot(left, rows_here) + dot(left_x, xpieces[plane])) / count
-        firsts[plane] = part
-        turned[pl.ds(pl.multiple_of(plane * width, width), width), :] = rows_here.T
-        return dot_t(halves(part), rows_here), dot_t(part.astype(bf16), xpieces[plane, 0:count])
-
-    started_parts = [begin(z)]
-    if len(zs) > 1:
-        hand_over(1)
-    if len(zs) > 2:
-        hand_over(2)
+
+    landed(z)
+    seen, along = begin([z])
     hand_corners()
-    started_parts += [begin(plane) for plane in zs]
-    seen = fold(functools.reduce(jnp.add, [part[0] for part in started_parts]))
-    along = functools.reduce(jnp.add, [part[1] for part in started_parts])
+    for n in range(1, len(zs)):
+        hand_over(n)
+    for group in (zs[:1], zs[1:]):
+        for plane in group:
+            landed(plane)
+        if group:
+            more_seen, more_along = begin(group)
+            seen, along = seen + more_seen, along + more_along
     drift = [firsts[k] for k in range(nz)]
 
     for t in range(NEWTON):
@@ -302,6 +308,8 @@
             left = halves(drive)
             left_x = halves(jnp.concatenate([pull, pull], axis=1))
             drift = [fold(dot(left, basis(k)) + dot(left_x, xpieces[k])) / count for k in range(nz)]
+            for k in range(nz):
+                firsts[k] = drift[k]
             seen, along = ahead(drift)
         shift = own_logits(seen)
         on_x = cross * kernel_sq * (along - row_sums(jnp.where(eye, along, 0.0)))
@@ -312,6 +320,8 @@
             / count
             for k in range(nz)
         ]
+        for k in range(nz):
+            seconds[k] = image[k]
         seen, along = ahead(image)
         shift_image = own_logits(seen)
         along = along - row_sums(jnp.where(eye, along, 0.0))
@@ -327,21 +337,23 @@
         curve_next = keep * keep * curve_total - 2.0 * keep * alpha * image_square + alpha * alpha * bent
         alpha_next = norm_next / curve_next
         on_drift, on_image = alpha + alpha_next * keep, -alpha_next * alpha
-        for k in range(nz):
-            firsts[k] = on_drift * drift[k] + on_image * image[k]
-        out_ref[t] = firsts[z, pl.ds(pl.multiple_of((core * chips + chip) * rows, rows), rows), :]
+        mine = pl.ds(pl.multiple_of((core * chips + chip) * rows, rows), rows)
+        out_ref[t] = on_drift * firsts[z, mine, :] + on_image * seconds[z, mine, :]
         if not last:
+            step_drift, step_image = move_size * on_drift, move_size * on_image
             for k in range(nz):
-                place[k] = place[k] + move_size * firsts[k]
-            logits = logits + move_size * (on_drift * shift + on_image * shift_image)
+                place[k] = place[k] + step_drift * drift[k] + step_image * image[k]
+            logits = logits + step_drift * shift + step_image * shift_image
     wait_sent(lambda number: xs(0, number), "x", started["x"])
-    wait_sent(lambda number: rows_all.at[pl.ds(0, number)], "a", started["a"])
-    wait_sent(lambda number: rows_all.at[pl.ds(0, number)], "p", started["p"])
+
+    def wait_rows(extra):
+        wait_sent(lambda number: rows_all.at[pl.ds(0, number)], "a", started["a"] + extra)
+
     if square:
-
-        @pl.when(middle)
-        def _():
-            wait_sent(lambda number: rows_all.at[pl.ds(0, number)], "m", 2)
+        pl.when(middle)(lambda: wait_rows(2))
+        pl.when(jnp.logical_not(middle))(lambda: wait_rows(0))
+    else:
+        wait_rows(0)
 
 
 def solution(mesh):
@@ -364,13 +376,14 @@
                 pltpu.VMEM((nz, 2 * count, width), bf16),
                 pltpu.VMEM((nz, count, width), f32),
                 pltpu.VMEM((nz, count, width), f32),
+                pltpu.VMEM((nz, count, width), f32),
                 pltpu.VMEM(labels.shape, jnp.int32),
-                dma((nz, 2)),
-                dma((nz,)),
+                dma((nz + 1,)),
+                dma((1,)),
                 dma((nz, 3)),
                 dma((nz,)),
-                dma((4,)),
-                dma((2 + width // LANES,)),
+                dma((2,)),
+                dma((3,)),
             ],
             compiler_params=pltpu.CompilerParams(collective_id=0, has_side_effects=True, vmem_limit_bytes=67_000_000),
         )(particles, data_rows.reshape(draws, width), labels)

time: 24.4 us -> 23.7 us (0.971)
  Pallas kernels: 23.6 us -> 22.9 us
    pallas_call x1, Pallas kernels: 23.6 us -> 22.9 us  [per_device(): pl.pallas_call(functools.partial(steps, nd, nz), out_shape=pltpu.VMEM((NE...]
where the time goes in v5:
time: 23.7 us; the launch traced here: 23.5 us
  Pallas kernels  22.9 us (97%)
  local copies, waits for them, and re-layouts  0.61 us (3%)
    pallas_call x1, Pallas kernels, per_device(): pl.pallas_call(functools.partial(steps, nd, nz), out_shape=pltpu.VMEM((NE...  22.9 us
    unnamed x1, local copies, waits for them, and re-layouts  0.61 us

profile of v5, /device:TPU:1, one launch (start us, length us, event | category | flops | bytes accessed | tf_op | source)
XLA Modules:
  0.0 23.5 jit_solution(7019595556879287451)
XLA Ops:
  0.0 22.9 %shard_map.37 = f32[2,8,256]{2,1,0:T(8,128)S(1)} custom-call(f32[8,256]{1,0:T(8,128)} %x_ref.1, bf16[128,256]{1,0:T(8,128)(2,1)} %bitcast.1, s32[8,16]{1,0:T(8,128)} %y_ref.1), custom_call_target="tpu_custom_call" | custom-call | tf_op jit(solution)/shard_map/pallas_call | solution.py:367
  22.9 0.6 %copy.5 = f32[2,8,256]{2,1,0:T(8,128)} copy(f32[2,8,256]{2,1,0:T(8,128)S(1)} %shard_map.37) | data formatting | bytes 32768

commit v6 on v5

--- a/solution.py
+++ b/solution.py
@@ -224,7 +224,7 @@
             weight.append(wide * wide * curve[g : g + 1])
         pull = (-prior_precision - 2.0 / scale) * kernel + jnp.where(eye, (2.0 / scale) * row_sums(kernel), 0.0)
         drive, weight = jnp.concatenate(drive, axis=1), jnp.concatenate(weight, axis=1)
-        return kernel_sq, row_sums(kernel_sq), weight, drive, pull
+        return kernel, gap, kernel_sq, row_sums(kernel_sq), weight, drive, pull
 
     def basis(k):
         return rows_all[pl.ds(k * nd, nd)].reshape(cols, width)
@@ -233,6 +233,16 @@
         seen = dot(jnp.concatenate([halves(v) for v in parts], axis=1), turned[...])
         along = functools.reduce(jnp.add, [dot_t(parts[k].astype(bf16), xpieces[k, 0:count]) for k in range(nz)])
         return fold(seen), along
+
+    def own_rows(values):
+        lines = []
+        for g in range(nd):
+            line = [jnp.zeros((rows, g * draws), f32)] if g > 0 else []
+            line.append(jnp.where(own_block, values[g : g + 1], 0.0))
+            if g + 1 < nd:
+                line.append(jnp.zeros((rows, cols - (g + 1) * draws), f32))
+            lines.append(jnp.concatenate(line, axis=1))
+        return jnp.concatenate(lines, axis=0)
 
     def own_logits(seen):
         return jnp.concatenate(
@@ -270,7 +280,7 @@
     logits = functools.reduce(jnp.add, [messages(k, blocks * rows) for k in range(nz)])
     targets = messages(0, blocks * rows + 1)
 
-    kernel_sq, total_sq, weight, drive, pull = prepare(logits)
+    _, _, kernel_sq, total_sq, weight, drive, pull = prepare(logits)
     left = halves(drive)
     left_x = halves(jnp.concatenate([pull, pull], axis=1))
 
@@ -304,10 +314,12 @@
     for t in range(NEWTON):
         last = t + 1 == NEWTON
         if t > 0:
-            kernel_sq, total_sq, weight, drive, pull = prepare(logits)
-            left = halves(drive)
-            left_x = halves(jnp.concatenate([pull, pull], axis=1))
-            drift = [fold(dot(left, basis(k)) + dot(left_x, xpieces[k])) / count for k in range(nz)]
+            kernel, gap, kernel_sq, total_sq, weight, _, _ = prepare(logits)
+            left = halves(own_rows(gap))
+            left_x = halves(jnp.concatenate([kernel, kernel], axis=1))
+            inward, outward = prior_precision + 2.0 / scale, (2.0 / scale) * row_sums(kernel)
+            pulled = [halves(fold(dot(left, basis(k))) - inward * place[k]) for k in range(nz)]
+            drift = [(fold(dot(left_x, pulled[k])) + outward * place[k]) / count for k in range(nz)]
             for k in range(nz):
                 firsts[k] = drift[k]
             seen, along = ahead(drift)

time: 23.7 us -> 23.5 us (level)
  no operation moved by 1% of the time
where the time goes in v6:
time: 23.5 us; the launch traced here: 23.3 us
  Pallas kernels  22.7 us (97%)
  local copies, waits for them, and re-layouts  0.61 us (3%)
    pallas_call x1, Pallas kernels, per_device(): pl.pallas_call(functools.partial(steps, nd, nz), out_shape=pltpu.VMEM((NE...  22.7 us
    unnamed x1, local copies, waits for them, and re-layouts  0.61 us

profile of v6, /device:TPU:1, one launch (start us, length us, event | category | flops | bytes accessed | tf_op | source)
XLA Modules:
  0.0 23.3 jit_solution(11350953568848812932)
XLA Ops:
  0.0 22.7 %shard_map.37 = f32[2,8,256]{2,1,0:T(8,128)S(1)} custom-call(f32[8,256]{1,0:T(8,128)} %x_ref.1, bf16[128,256]{1,0:T(8,128)(2,1)} %bitcast.1, s32[8,16]{1,0:T(8,128)} %y_ref.1), custom_call_target="tpu_custom_call" | custom-call | tf_op jit(solution)/shard_map/pallas_call | solution.py:379
  22.7 0.6 %copy.5 = f32[2,8,256]{2,1,0:T(8,128)} copy(f32[2,8,256]{2,1,0:T(8,128)S(1)} %shard_map.37) | data formatting | bytes 32768

commit v7 on v6

--- a/solution.py
+++ b/solution.py
@@ -229,10 +229,11 @@
     def basis(k):
         return rows_all[pl.ds(k * nd, nd)].reshape(cols, width)
 
-    def ahead(parts):
-        seen = dot(jnp.concatenate([halves(v) for v in parts], axis=1), turned[...])
+    def ahead(parts, exact=True):
+        pieces = [halves(v) if exact else v.astype(bf16) for v in parts]
+        seen = dot(jnp.concatenate(pieces, axis=1), turned[...])
         along = functools.reduce(jnp.add, [dot_t(parts[k].astype(bf16), xpieces[k, 0:count]) for k in range(nz)])
-        return fold(seen), along
+        return fold(seen) if exact else seen, along
 
     def own_rows(values):
         lines = []
@@ -334,7 +335,7 @@
         ]
         for k in range(nz):
             seconds[k] = image[k]
-        seen, along = ahead(image)
+        seen, along = ahead(image, not last)
         shift_image = own_logits(seen)
         along = along - row_sums(jnp.where(eye, along, 0.0))
         norm = total_of(functools.reduce(jnp.add, [d * d for d in drift]))

time: 23.5 us -> 23.5 us (level)
  no operation moved by 1% of the time
where the time goes in v7:
time: 23.5 us; the launch traced here: 23.4 us
  Pallas kernels  22.8 us (97%)
  local copies, waits for them, and re-layouts  0.61 us (3%)
    pallas_call x1, Pallas kernels, per_device(): pl.pallas_call(functools.partial(steps, nd, nz), out_shape=pltpu.VMEM((NE...  22.8 us
    unnamed x1, local copies, waits for them, and re-layouts  0.61 us

profile of v7, /device:TPU:1, one launch (start us, length us, event | category | flops | bytes accessed | tf_op | source)
XLA Modules:
  0.0 23.4 jit_solution(5979382484399164760)
XLA Ops:
  0.0 22.8 %shard_map.37 = f32[2,8,256]{2,1,0:T(8,128)S(1)} custom-call(f32[8,256]{1,0:T(8,128)} %x_ref.1, bf16[128,256]{1,0:T(8,128)(2,1)} %bitcast.1, s32[8,16]{1,0:T(8,128)} %y_ref.1), custom_call_target="tpu_custom_call" | custom-call | tf_op jit(solution)/shard_map/pallas_call | solution.py:380
  22.8 0.6 %copy.5 = f32[2,8,256]{2,1,0:T(8,128)} copy(f32[2,8,256]{2,1,0:T(8,128)S(1)} %shard_map.37) | data formatting | bytes 32768
